TPU v7x, 256 devices: a whole 4x4x8 slice. The times are simulated.
256 devices in a mesh: section: 4 (over y), row: 8 (over x, core), col: 8 (over z).
Axes of the slice: x: 4, y: 4, z: 8, core: 2. Of those that a mesh axis runs over, the one named last changes fastest.
Arguments:
- cotangent: float32 [4, 128, 4096], P('section', None, ('row', 'col')), may hold values from -6 to 6
- incoming: float32 [4, 128, 4096], P('section', None, ('row', 'col')), may hold values from -6 to 6
- upd_u: float32 [4, 8, 128, 4096], P('section', None, None, ('row', 'col')), may hold values from -4 to 4
- upd_v: float32 [4, 8, 128, 4096], P('section', None, None, ('row', 'col')), may hold values from -0.0078125 to 0.0078125
- saved_x: bfloat16 [4, 4, 128, 4096], P('section', None, None, ('row', 'col')), may hold values from -6 to 6
- saved_h: bfloat16 [4, 4, 2, 128, 14336], P('section', None, None, None, 'col'), may hold values from -6 to 6
- norm_gain: float32 [4, 4096], P('section', ('row', 'col')), may hold values from 0.25 to 1.75
- w_gate: bfloat16 [4, 4096, 14336], P('section', 'row', 'col'), may hold values from -0.09375 to 0.09375
- w_up: bfloat16 [4, 4096, 14336], P('section', 'row', 'col'), may hold values from -0.09375 to 0.09375
- w_down: bfloat16 [4, 14336, 4096], P('section', 'col', 'row'), may hold values from -0.046875 to 0.046875
Outputs:
- new_cotangent: float32 [4, 128, 4096], P('section', None, ('row', 'col'))
- residual_out: float32 [4, 128, 4096], P('section', None, ('row', 'col'))
All inputs are finite; a program needn't handle non-finite values.
Results may differ from a plain program's by a relative error of at most 0.014.
Values may be sent and summed in bfloat16 or wider, within the bound.
A program may use at most 64 MiB of HBM per device.

v0:
```python
import jax
import jax.numpy as jnp
from jax import lax
from jax.sharding import PartitionSpec as P

D = 4096


eps = 1e-05


def shifted(x, axis, by):
    devices = lax.axis_size(axis)
    return lax.ppermute(x, axis, [(i, (i + by) % devices) for i in range(devices)])


def sent_to_all(x, axis):
    devices = lax.axis_size(axis)
    return lax.all_to_all(jnp.broadcast_to(x[None], (devices, *x.shape)), axis, 0, 0, tiled=True)


def of_everyone(x, axis):
    everything = sent_to_all(x, axis)
    return jnp.sum(everything, axis=0)


def joined_along(tiles, dim):
    dims = list(tiles.shape[1:])
    dims[dim] *= tiles.shape[0]
    return jnp.moveaxis(tiles, 0, dim).reshape(dims)


def gathered_copies(x, axis, dim):
    return joined_along(sent_to_all(x, axis), dim)


def split_up(x, dim, devices):
    before, after = (x.shape[:dim], x.shape[dim + 1 :])
    return jnp.moveaxis(x.reshape(*before, devices, -1, *after), dim, 0)


def summed_on_arrival(x, axis, dim):
    tiles = split_up(x, dim, lax.axis_size(axis))
    arrived = lax.all_to_all(tiles, axis, split_axis=0, concat_axis=0, tiled=True)
    return arrived.sum(axis=0)


def rows_first(arrays, axis, dims):
    turned = [jnp.moveaxis(a, dim, 0) for a, dim in zip(arrays, dims)]
    widths = [t[0].size for t in turned]
    both = jnp.concatenate([t.reshape(-1, w) for t, w in zip(turned, widths)], axis=1)
    out = lax.all_gather(both, axis, axis=0, tiled=True)
    tiles = jnp.split(out, [sum(widths[:k]) for k in range(1, len(widths))], axis=1)
    return tuple(
        (
            jnp.moveaxis(b.reshape(-1, *t.shape[1:]), 0, dim)
            for b, t, dim in zip(tiles, turned, dims)
        )
    )


def rotate(carry):
    return shifted(carry, "section", -1)


def shards(cotangent, incoming, upd_u, upd_v, saved_x, saved_h, norm_gain, w_gate, w_up, w_down):
    sections = lax.axis_size("section")
    section_idx = lax.axis_index("section")
    inputs_all = saved_x[0].astype(jnp.float32)
    hidden_all = saved_h[0]
    gain = norm_gain[0]
    wg = w_gate[0]
    wu = w_up[0]
    wd = w_down[0]
    sq_all = of_everyone(jnp.sum(inputs_all * inputs_all, axis=2), ("row", "col"))

    def layer_step(step, carry):
        carry = rotate(carry)
        micro = (section_idx + step + 1) % sections
        xf = lax.dynamic_index_in_dim(inputs_all, micro, 0, keepdims=False)
        hpair = lax.dynamic_index_in_dim(hidden_all, micro, 0, keepdims=False)
        sumsq = lax.dynamic_index_in_dim(sq_all, micro, 0, keepdims=False)
        gy = carry.astype(jnp.bfloat16)
        wide = gathered_copies(gy, "col", 1)
        ga_part = lax.dot_general(
            wide, wd, (((1,), (1,)), ((), ())), preferred_element_type=jnp.float32
        )
        ga = summed_on_arrival(ga_part, "row", 1)
        width = ga.shape[1]
        offset = lax.axis_index("row") * width
        hg = lax.dynamic_slice_in_dim(hpair[0], offset, width, 1).astype(jnp.float32)
        hu = lax.dynamic_slice_in_dim(hpair[1], offset, width, 1).astype(jnp.float32)
        sig = jax.nn.sigmoid(hg)
        part_gate = (ga * hu * sig * (1.0 + hg * (1.0 - sig))).astype(jnp.bfloat16)
        part_up = (ga * hg * sig).astype(jnp.bfloat16)
        grad_gate, grad_up = rows_first((part_gate, part_up), "row", (1, 1))
        first = lax.dot_general(
            wg, grad_gate, (((1,), (1,)), ((), ())), preferred_element_type=jnp.float32
        )
        second = lax.dot_general(
            wu, grad_up, (((1,), (1,)), ((), ())), preferred_element_type=jnp.float32
        )
        normgrad = summed_on_arrival(first + second, "col", 0).T
        rstd = lax.rsqrt(sumsq / D + eps)[:, None]
        scaled = gain * normgrad
        inner = of_everyone(jnp.sum(scaled * xf, axis=1), ("row", "col"))[:, None] / D
        updated = carry + rstd * scaled - xf * (rstd * rstd * rstd) * inner
        active = jnp.logical_and(step >= micro, step - micro < sections)
        return jnp.where(active, updated, carry)

    pulled = lax.fori_loop(0, 2 * sections - 1, layer_step, cotangent[0])
    pulled = rotate(pulled)
    resid = pulled + incoming[0] - cotangent[0]
    local_dots = jnp.einsum("urd,rd->u", upd_v[0], resid)
    dots = of_everyone(local_dots, ("row", "col"))
    update = jnp.einsum("u,urd->rd", dots, upd_u[0])
    fresh = cotangent[0] + resid - update
    return (fresh[None], resid[None])


def solution(mesh):
    placed = (
        P("section", None, ("row", "col")),
        P("section", None, ("row", "col")),
        P("section", None, None, ("row", "col")),
        P("section", None, None, ("row", "col")),
        P("section", None, None, ("row", "col")),
        P("section", None, None, None, "col"),
        P("section", ("row", "col")),
        P("section", "row", "col"),
        P("section", "row", "col"),
        P("section", "col", "row"),
    )
    return jax.shard_map(
        shards,
        mesh=mesh,
        in_specs=placed,
        out_specs=(P("section", None, ("row", "col")), P("section", None, ("row", "col"))),
        check_vma=False,
    )
```

profile of v0, /device:TPU:1, one launch (start us, length us, event | category | flops | bytes accessed | tf_op | source)
XLA Modules:
  0.0 648.4 jit_solution(8685798725237322792)
XLA Ops:
  2.2 13.0 %all-to-all-start.4 = ((f32[64,4,128]{2,1,0:T(4,128)}), f32[64,4,128]{2,1,0:T(4,128)S(1)}, u32[]{:S(2)}, u32[]{:S(2)}) async-start(f32[64,4,128]{2,1,0:T(4,128)} %broadcast_in_dim.57), calls=%async_computation.4 | async-start | bytes 262144 | tf_op jit(solution)/shard_map/all_to_all | solution.py:19
  16.0 6.0 copy.27
  25.3 602.3 %while.15 = (s32[]{:T(128)}, f32[128,64]{0,1:T(8,128)S(1)}, s32[]{:T(128)}, f32[4,128]{1,0:T(4,128)S(1)}, f32[1,64]{1,0:T(1,128)S(1)}, /*index=5*/bf16[1792,512]...) while((s32[]{:T(128)}, f32[128,64]{0,1:T(8,128)S(1)}, ...), condition=%wide.region_7.8_spmd, body=%wide.region_2.7_spmd.sunk | while | flops 705724800 | bytes 23550628 | solution.py:111
  29.2 11.2 %all_to_all.65 = bf16[8,128,64]{1,2,0:T(8,128)(2,1)S(1)} all-to-all(bf16[8,128,64]{1,2,0:T(8,128)(2,1)S(1)} %broadcast_in_dim.63), channel_id=1, replica_groups=mesh['section'=4,'row'=8,'col'=8] {'col'}, dimensions={0} | all-to-all | bytes 262144 | tf_op jit(solution)/shard_map/while/body/eval_jaxpr/all_to_all | solution.py:19
  43.4 7.0 %all-to-all-start.1 = ((f32[8,128,224]{1,2,0:T(8,128)}), f32[8,128,224]{1,2,0:T(8,128)S(1)}, u32[]{:S(2)}, u32[]{:S(2)}) async-start(f32[8,128,224]{1,2,0:T(8,128)} %convolution_bitcast_fusion.3), calls=%async_computation.1 | async-start | bytes 1835008 | tf_op jit(solution)/shard_map/while/body/eval_jaxpr/all_to_all | solution.py:44
  50.4 13.6 %all-to-all-done.1 = f32[8,128,224]{1,2,0:T(8,128)S(1)} async-done(((f32[8,128,224]{1,2,0:T(8,128)}), f32[8,128,224]{1,2,0:T(8,128)S(1)}, u32[]{:S(2)}, u32[]{:S(2)}) %all-to-all-start.1) | async-done | bytes 917536 | tf_op jit(solution)/shard_map/while/body/eval_jaxpr/all_to_all | solution.py:44
  65.0 14.6 %all_gather.11 = bf16[1792,256]{1,0:T(8,128)(2,1)S(1)} all-gather(bf16[224,256]{1,0:T(8,128)(2,1)S(1)} %pad_maximum_fusion.2), channel_id=1, replica_groups=mesh['section'=4,'row'=8,'col'=8] {'row'}, dimensions={0}, use_global_device_ids=true | all-gather | bytes 1032192 | tf_op jit(solution)/shard_map/while/body/eval_jaxpr/all_gather | solution.py:52
  81.9 3.4 all-to-all-start.2
  85.3 12.3 %all-to-all-done.2 = f32[8,64,128]{2,1,0:T(8,128)S(1)} async-done(((f32[8,64,128]{2,1,0:T(8,128)}), f32[8,64,128]{2,1,0:T(8,128)S(1)}, u32[]{:S(2)}, u32[]{:S(2)}) %all-to-all-start.2) | async-done | bytes 262176 | tf_op jit(solution)/shard_map/while/body/eval_jaxpr/all_to_all | solution.py:44
  98.3 4.5 all-to-all-start.3
  102.9 9.2 %all-to-all-done.3 = f32[64,1,128]{2,1,0:T(1,128)S(1)} async-done(((f32[64,1,128]{2,1,0:T(1,128)}), f32[64,1,128]{2,1,0:T(1,128)S(1)}, u32[]{:S(2)}, u32[]{:S(2)}) %all-to-all-start.3) | async-done | bytes 32800 | tf_op jit(solution)/shard_map/while/body/eval_jaxpr/all_to_all | solution.py:19
  112.2 3.3 collective-permute-start
  116.6 10.3 %all_to_all.65 = bf16[8,128,64]{1,2,0:T(8,128)(2,1)S(1)} all-to-all(bf16[8,128,64]{1,2,0:T(8,128)(2,1)S(1)} %broadcast_in_dim.63), channel_id=1, replica_groups=mesh['section'=4,'row'=8,'col'=8] {'col'}, dimensions={0} | all-to-all | bytes 262144 | tf_op jit(solution)/shard_map/while/body/eval_jaxpr/all_to_all | solution.py:19
  130.0 6.3 all-to-all-start.1
  136.3 13.6 %all-to-all-done.1 = f32[8,128,224]{1,2,0:T(8,128)S(1)} async-done(((f32[8,128,224]{1,2,0:T(8,128)}), f32[8,128,224]{1,2,0:T(8,128)S(1)}, u32[]{:S(2)}, u32[]{:S(2)}) %all-to-all-start.1) | async-done | bytes 917536 | tf_op jit(solution)/shard_map/while/body/eval_jaxpr/all_to_all | solution.py:44
  150.9 14.6 %all_gather.11 = bf16[1792,256]{1,0:T(8,128)(2,1)S(1)} all-gather(bf16[224,256]{1,0:T(8,128)(2,1)S(1)} %pad_maximum_fusion.2), channel_id=1, replica_groups=mesh['section'=4,'row'=8,'col'=8] {'row'}, dimensions={0}, use_global_device_ids=true | all-gather | bytes 1032192 | tf_op jit(solution)/shard_map/while/body/eval_jaxpr/all_gather | solution.py:52
  167.8 3.4 all-to-all-start.2
  171.2 12.3 %all-to-all-done.2 = f32[8,64,128]{2,1,0:T(8,128)S(1)} async-done(((f32[8,64,128]{2,1,0:T(8,128)}), f32[8,64,128]{2,1,0:T(8,128)S(1)}, u32[]{:S(2)}, u32[]{:S(2)}) %all-to-all-start.2) | async-done | bytes 262176 | tf_op jit(solution)/shard_map/while/body/eval_jaxpr/all_to_all | solution.py:44
  184.2 4.5 all-to-all-start.3
  188.8 9.2 %all-to-all-done.3 = f32[64,1,128]{2,1,0:T(1,128)S(1)} async-done(((f32[64,1,128]{2,1,0:T(1,128)}), f32[64,1,128]{2,1,0:T(1,128)S(1)}, u32[]{:S(2)}, u32[]{:S(2)}) %all-to-all-start.3) | async-done | bytes 32800 | tf_op jit(solution)/shard_map/while/body/eval_jaxpr/all_to_all | solution.py:19
  202.5 10.3 %all_to_all.65 = bf16[8,128,64]{1,2,0:T(8,128)(2,1)S(1)} all-to-all(bf16[8,128,64]{1,2,0:T(8,128)(2,1)S(1)} %broadcast_in_dim.63), channel_id=1, replica_groups=mesh['section'=4,'row'=8,'col'=8] {'col'}, dimensions={0} | all-to-all | bytes 262144 | tf_op jit(solution)/shard_map/while/body/eval_jaxpr/all_to_all | solution.py:19
  215.9 6.3 all-to-all-start.1
  222.2 13.6 %all-to-all-done.1 = f32[8,128,224]{1,2,0:T(8,128)S(1)} async-done(((f32[8,128,224]{1,2,0:T(8,128)}), f32[8,128,224]{1,2,0:T(8,128)S(1)}, u32[]{:S(2)}, u32[]{:S(2)}) %all-to-all-start.1) | async-done | bytes 917536 | tf_op jit(solution)/shard_map/while/body/eval_jaxpr/all_to_all | solution.py:44
  236.8 14.6 %all_gather.11 = bf16[1792,256]{1,0:T(8,128)(2,1)S(1)} all-gather(bf16[224,256]{1,0:T(8,128)(2,1)S(1)} %pad_maximum_fusion.2), channel_id=1, replica_groups=mesh['section'=4,'row'=8,'col'=8] {'row'}, dimensions={0}, use_global_device_ids=true | all-gather | bytes 1032192 | tf_op jit(solution)/shard_map/while/body/eval_jaxpr/all_gather | solution.py:52
  253.7 3.4 all-to-all-start.2
  257.1 12.3 %all-to-all-done.2 = f32[8,64,128]{2,1,0:T(8,128)S(1)} async-done(((f32[8,64,128]{2,1,0:T(8,128)}), f32[8,64,128]{2,1,0:T(8,128)S(1)}, u32[]{:S(2)}, u32[]{:S(2)}) %all-to-all-start.2) | async-done | bytes 262176 | tf_op jit(solution)/shard_map/while/body/eval_jaxpr/all_to_all | solution.py:44
  270.1 4.5 all-to-all-start.3
  274.7 9.2 %all-to-all-done.3 = f32[64,1,128]{2,1,0:T(1,128)S(1)} async-done(((f32[64,1,128]{2,1,0:T(1,128)}), f32[64,1,128]{2,1,0:T(1,128)S(1)}, u32[]{:S(2)}, u32[]{:S(2)}) %all-to-all-start.3) | async-done | bytes 32800 | tf_op jit(solution)/shard_map/while/body/eval_jaxpr/all_to_all | solution.py:19
  288.4 10.3 %all_to_all.65 = bf16[8,128,64]{1,2,0:T(8,128)(2,1)S(1)} all-to-all(bf16[8,128,64]{1,2,0:T(8,128)(2,1)S(1)} %broadcast_in_dim.63), channel_id=1, replica_groups=mesh['section'=4,'row'=8,'col'=8] {'col'}, dimensions={0} | all-to-all | bytes 262144 | tf_op jit(solution)/shard_map/while/body/eval_jaxpr/all_to_all | solution.py:19
  301.8 6.3 all-to-all-start.1
  308.1 13.6 %all-to-all-done.1 = f32[8,128,224]{1,2,0:T(8,128)S(1)} async-done(((f32[8,128,224]{1,2,0:T(8,128)}), f32[8,128,224]{1,2,0:T(8,128)S(1)}, u32[]{:S(2)}, u32[]{:S(2)}) %all-to-all-start.1) | async-done | bytes 917536 | tf_op jit(solution)/shard_map/while/body/eval_jaxpr/all_to_all | solution.py:44
  322.7 14.6 %all_gather.11 = bf16[1792,256]{1,0:T(8,128)(2,1)S(1)} all-gather(bf16[224,256]{1,0:T(8,128)(2,1)S(1)} %pad_maximum_fusion.2), channel_id=1, replica_groups=mesh['section'=4,'row'=8,'col'=8] {'row'}, dimensions={0}, use_global_device_ids=true | all-gather | bytes 1032192 | tf_op jit(solution)/shard_map/while/body/eval_jaxpr/all_gather | solution.py:52
  339.5 3.4 all-to-all-start.2
  343.0 12.3 %all-to-all-done.2 = f32[8,64,128]{2,1,0:T(8,128)S(1)} async-done(((f32[8,64,128]{2,1,0:T(8,128)}), f32[8,64,128]{2,1,0:T(8,128)S(1)}, u32[]{:S(2)}, u32[]{:S(2)}) %all-to-all-start.2) | async-done | bytes 262176 | tf_op jit(solution)/shard_map/while/body/eval_jaxpr/all_to_all | solution.py:44
  356.0 4.5 all-to-all-start.3
  360.6 9.2 %all-to-all-done.3 = f32[64,1,128]{2,1,0:T(1,128)S(1)} async-done(((f32[64,1,128]{2,1,0:T(1,128)}), f32[64,1,128]{2,1,0:T(1,128)S(1)}, u32[]{:S(2)}, u32[]{:S(2)}) %all-to-all-start.3) | async-done | bytes 32800 | tf_op jit(solution)/shard_map/while/body/eval_jaxpr/all_to_all | solution.py:19
  369.9 3.3 collective-permute-start
  374.3 10.3 %all_to_all.65 = bf16[8,128,64]{1,2,0:T(8,128)(2,1)S(1)} all-to-all(bf16[8,128,64]{1,2,0:T(8,128)(2,1)S(1)} %broadcast_in_dim.63), channel_id=1, replica_groups=mesh['section'=4,'row'=8,'col'=8] {'col'}, dimensions={0} | all-to-all | bytes 262144 | tf_op jit(solution)/shard_map/while/body/eval_jaxpr/all_to_all | solution.py:19
  387.7 6.3 all-to-all-start.1
  393.9 13.6 %all-to-all-done.1 = f32[8,128,224]{1,2,0:T(8,128)S(1)} async-done(((f32[8,128,224]{1,2,0:T(8,128)}), f32[8,128,224]{1,2,0:T(8,128)S(1)}, u32[]{:S(2)}, u32[]{:S(2)}) %all-to-all-start.1) | async-done | bytes 917536 | tf_op jit(solution)/shard_map/while/body/eval_jaxpr/all_to_all | solution.py:44
  408.6 14.6 %all_gather.11 = bf16[1792,256]{1,0:T(8,128)(2,1)S(1)} all-gather(bf16[224,256]{1,0:T(8,128)(2,1)S(1)} %pad_maximum_fusion.2), channel_id=1, replica_groups=mesh['section'=4,'row'=8,'col'=8] {'row'}, dimensions={0}, use_global_device_ids=true | all-gather | bytes 1032192 | tf_op jit(solution)/shard_map/while/body/eval_jaxpr/all_gather | solution.py:52
  425.4 3.4 all-to-all-start.2
  428.9 12.3 %all-to-all-done.2 = f32[8,64,128]{2,1,0:T(8,128)S(1)} async-done(((f32[8,64,128]{2,1,0:T(8,128)}), f32[8,64,128]{2,1,0:T(8,128)S(1)}, u32[]{:S(2)}, u32[]{:S(2)}) %all-to-all-start.2) | async-done | bytes 262176 | tf_op jit(solution)/shard_map/while/body/eval_jaxpr/all_to_all | solution.py:44
  441.9 4.5 all-to-all-start.3
  446.5 9.2 %all-to-all-done.3 = f32[64,1,128]{2,1,0:T(1,128)S(1)} async-done(((f32[64,1,128]{2,1,0:T(1,128)}), f32[64,1,128]{2,1,0:T(1,128)S(1)}, u32[]{:S(2)}, u32[]{:S(2)}) %all-to-all-start.3) | async-done | bytes 32800 | tf_op jit(solution)/shard_map/while/body/eval_jaxpr/all_to_all | solution.py:19
  455.8 3.3 collective-permute-start
  460.2 10.3 %all_to_all.65 = bf16[8,128,64]{1,2,0:T(8,128)(2,1)S(1)} all-to-all(bf16[8,128,64]{1,2,0:T(8,128)(2,1)S(1)} %broadcast_in_dim.63), channel_id=1, replica_groups=mesh['section'=4,'row'=8,'col'=8] {'col'}, dimensions={0} | all-to-all | bytes 262144 | tf_op jit(solution)/shard_map/while/body/eval_jaxpr/all_to_all | solution.py:19
  473.5 6.3 all-to-all-start.1
  479.8 13.6 %all-to-all-done.1 = f32[8,128,224]{1,2,0:T(8,128)S(1)} async-done(((f32[8,128,224]{1,2,0:T(8,128)}), f32[8,128,224]{1,2,0:T(8,128)S(1)}, u32[]{:S(2)}, u32[]{:S(2)}) %all-to-all-start.1) | async-done | bytes 917536 | tf_op jit(solution)/shard_map/while/body/eval_jaxpr/all_to_all | solution.py:44
  494.4 14.6 %all_gather.11 = bf16[1792,256]{1,0:T(8,128)(2,1)S(1)} all-gather(bf16[224,256]{1,0:T(8,128)(2,1)S(1)} %pad_maximum_fusion.2), channel_id=1, replica_groups=mesh['section'=4,'row'=8,'col'=8] {'row'}, dimensions={0}, use_global_device_ids=true | all-gather | bytes 1032192 | tf_op jit(solution)/shard_map/while/body/eval_jaxpr/all_gather | solution.py:52
  511.3 3.4 all-to-all-start.2
  514.7 12.3 %all-to-all-done.2 = f32[8,64,128]{2,1,0:T(8,128)S(1)} async-done(((f32[8,64,128]{2,1,0:T(8,128)}), f32[8,64,128]{2,1,0:T(8,128)S(1)}, u32[]{:S(2)}, u32[]{:S(2)}) %all-to-all-start.2) | async-done | bytes 262176 | tf_op jit(solution)/shard_map/while/body/eval_jaxpr/all_to_all | solution.py:44
  527.8 4.5 all-to-all-start.3
  532.3 9.2 %all-to-all-done.3 = f32[64,1,128]{2,1,0:T(1,128)S(1)} async-done(((f32[64,1,128]{2,1,0:T(1,128)}), f32[64,1,128]{2,1,0:T(1,128)S(1)}, u32[]{:S(2)}, u32[]{:S(2)}) %all-to-all-start.3) | async-done | bytes 32800 | tf_op jit(solution)/shard_map/while/body/eval_jaxpr/all_to_all | solution.py:19
  546.0 10.3 %all_to_all.65 = bf16[8,128,64]{1,2,0:T(8,128)(2,1)S(1)} all-to-all(bf16[8,128,64]{1,2,0:T(8,128)(2,1)S(1)} %broadcast_in_dim.63), channel_id=1, replica_groups=mesh['section'=4,'row'=8,'col'=8] {'col'}, dimensions={0} | all-to-all | bytes 262144 | tf_op jit(solution)/shard_map/while/body/eval_jaxpr/all_to_all | solution.py:19
  559.4 6.3 all-to-all-start.1
  565.7 13.6 %all-to-all-done.1 = f32[8,128,224]{1,2,0:T(8,128)S(1)} async-done(((f32[8,128,224]{1,2,0:T(8,128)}), f32[8,128,224]{1,2,0:T(8,128)S(1)}, u32[]{:S(2)}, u32[]{:S(2)}) %all-to-all-start.1) | async-done | bytes 917536 | tf_op jit(solution)/shard_map/while/body/eval_jaxpr/all_to_all | solution.py:44
  580.3 14.6 %all_gather.11 = bf16[1792,256]{1,0:T(8,128)(2,1)S(1)} all-gather(bf16[224,256]{1,0:T(8,128)(2,1)S(1)} %pad_maximum_fusion.2), channel_id=1, replica_groups=mesh['section'=4,'row'=8,'col'=8] {'row'}, dimensions={0}, use_global_device_ids=true | all-gather | bytes 1032192 | tf_op jit(solution)/shard_map/while/body/eval_jaxpr/all_gather | solution.py:52
  597.2 3.4 all-to-all-start.2
  600.6 12.3 %all-to-all-done.2 = f32[8,64,128]{2,1,0:T(8,128)S(1)} async-done(((f32[8,64,128]{2,1,0:T(8,128)}), f32[8,64,128]{2,1,0:T(8,128)S(1)}, u32[]{:S(2)}, u32[]{:S(2)}) %all-to-all-start.2) | async-done | bytes 262176 | tf_op jit(solution)/shard_map/while/body/eval_jaxpr/all_to_all | solution.py:44
  613.7 4.5 all-to-all-start.3
  618.2 9.2 %all-to-all-done.3 = f32[64,1,128]{2,1,0:T(1,128)S(1)} async-done(((f32[64,1,128]{2,1,0:T(1,128)}), f32[64,1,128]{2,1,0:T(1,128)S(1)}, u32[]{:S(2)}, u32[]{:S(2)}) %all-to-all-start.3) | async-done | bytes 32800 | tf_op jit(solution)/shard_map/while/body/eval_jaxpr/all_to_all | solution.py:19
  627.6 3.3 collective-permute-start.1
  633.2 14.3 %all_to_all.64 = f32[64,1,8]{2,1,0:T(1,128)S(1)} all-to-all(f32[64,1,8]{2,1,0:T(1,128)S(1)} %broadcast_in_dim.58), channel_id=1, replica_groups=mesh['section'=4,'row'=8,'col'=8] {'row','col'}, dimensions={0} | all-to-all | bytes 4096 | tf_op jit(solution)/shard_map/all_to_all | solution.py:19
  (164 shorter events, 79.6 us)
Async XLA Ops:
  0.6 646.9 %copy-start = (f32[1,8,128,64]{2,3,1,0:T(8,128)S(1)}, f32[1,8,128,64]{2,3,1,0:T(8,128)}, u32[]{:S(2)}) copy-start(f32[1,8,128,64]{2,3,1,0:T(8,128)} %param.14) | copy-start | bytes 786436
  2.2 22.9 %all-to-all-start.4 = ((f32[64,4,128]{2,1,0:T(4,128)}), f32[64,4,128]{2,1,0:T(4,128)S(1)}, u32[]{:S(2)}, u32[]{:S(2)}) async-start(f32[64,4,128]{2,1,0:T(4,128)} %broadcast_in_dim.57), calls=%async_computation.4 | async-start | bytes 262144 | tf_op jit(solution)/shard_map/all_to_all | solution.py:19
  16.0 6.1 copy-start.4
  16.0 9.3 %copy-start.1 = (bf16[1,512,1792]{2,1,0:T(8,128)(2,1)S(1)}, bf16[1,512,1792]{2,1,0:T(8,128)(2,1)}, u32[]{:S(2)}) copy-start(bf16[1,512,1792]{2,1,0:T(8,128)(2,1)} %param.19) | copy-start | bytes 5505028
  16.0 9.3 %copy-start.6 = (f32[1,64]{1,0:T(1,128)S(1)}, f32[1,64]{1,0:T(1,128)}, u32[]{:S(2)}) copy-start(f32[1,64]{1,0:T(1,128)} %param.18) | copy-start | bytes 772
  25.3 606.6 %copy-start.3 = (f32[1,128,64]{1,2,0:T(8,128)S(1)}, f32[1,128,64]{1,2,0:T(8,128)}, u32[]{:S(2)}) copy-start(f32[1,128,64]{1,2,0:T(8,128)} %param.12) | copy-start | bytes 98308
  25.3 606.6 %copy-start.7 = (f32[1,128,64]{1,2,0:T(8,128)S(1)}, f32[1,128,64]{1,2,0:T(8,128)}, u32[]{:S(2)}) copy-start(f32[1,128,64]{1,2,0:T(8,128)} %param.13) | copy-start | bytes 98308
  25.3 3.8 collective-permute-start
  43.4 20.6 %all-to-all-start.1 = ((f32[8,128,224]{1,2,0:T(8,128)}), f32[8,128,224]{1,2,0:T(8,128)S(1)}, u32[]{:S(2)}, u32[]{:S(2)}) async-start(f32[8,128,224]{1,2,0:T(8,128)} %convolution_bitcast_fusion.3), calls=%async_computation.1 | async-start | bytes 1835008 | tf_op jit(solution)/shard_map/while/body/eval_jaxpr/all_to_all | solution.py:44
  65.0 15.3 %copy-start.2 = (bf16[512,1792]{1,0:T(8,128)(2,1)S(1)}, bf16[512,1792]{1,0:T(8,128)(2,1)}, u32[]{:S(2)}) copy-start(bf16[512,1792]{1,0:T(8,128)(2,1)} %get-tuple-element.397) | copy-start | bytes 5505028 | tf_op jit(solution)/shard_map/while
  81.9 15.7 %all-to-all-start.2 = ((f32[8,64,128]{2,1,0:T(8,128)}), f32[8,64,128]{2,1,0:T(8,128)S(1)}, u32[]{:S(2)}, u32[]{:S(2)}) async-start(f32[8,64,128]{2,1,0:T(8,128)} %bitcast.122), calls=%async_computation.2 | async-start | bytes 524288 | tf_op jit(solution)/shard_map/while/body/eval_jaxpr/all_to_all | solution.py:44
  98.3 13.8 %all-to-all-start.3 = ((f32[64,1,128]{2,1,0:T(1,128)}), f32[64,1,128]{2,1,0:T(1,128)S(1)}, u32[]{:S(2)}, u32[]{:S(2)}) async-start(f32[64,1,128]{2,1,0:T(1,128)} %broadcast_in_dim.64), calls=%async_computation.3 | async-start | bytes 65536 | tf_op jit(solution)/shard_map/while/body/eval_jaxpr/all_to_all | solution.py:19
  112.2 4.4 collective-permute-start
  130.0 19.9 %all-to-all-start.1 = ((f32[8,128,224]{1,2,0:T(8,128)}), f32[8,128,224]{1,2,0:T(8,128)S(1)}, u32[]{:S(2)}, u32[]{:S(2)}) async-start(f32[8,128,224]{1,2,0:T(8,128)} %convolution_bitcast_fusion.3), calls=%async_computation.1 | async-start | bytes 1835008 | tf_op jit(solution)/shard_map/while/body/eval_jaxpr/all_to_all | solution.py:44
  150.9 15.3 %copy-start.2 = (bf16[512,1792]{1,0:T(8,128)(2,1)S(1)}, bf16[512,1792]{1,0:T(8,128)(2,1)}, u32[]{:S(2)}) copy-start(bf16[512,1792]{1,0:T(8,128)(2,1)} %get-tuple-element.397) | copy-start | bytes 5505028 | tf_op jit(solution)/shard_map/while
  167.8 15.7 %all-to-all-start.2 = ((f32[8,64,128]{2,1,0:T(8,128)}), f32[8,64,128]{2,1,0:T(8,128)S(1)}, u32[]{:S(2)}, u32[]{:S(2)}) async-start(f32[8,64,128]{2,1,0:T(8,128)} %bitcast.122), calls=%async_computation.2 | async-start | bytes 524288 | tf_op jit(solution)/shard_map/while/body/eval_jaxpr/all_to_all | solution.py:44
  184.2 13.8 %all-to-all-start.3 = ((f32[64,1,128]{2,1,0:T(1,128)}), f32[64,1,128]{2,1,0:T(1,128)S(1)}, u32[]{:S(2)}, u32[]{:S(2)}) async-start(f32[64,1,128]{2,1,0:T(1,128)} %broadcast_in_dim.64), calls=%async_computation.3 | async-start | bytes 65536 | tf_op jit(solution)/shard_map/while/body/eval_jaxpr/all_to_all | solution.py:19
  198.1 4.3 collective-permute-start
  215.9 19.9 %all-to-all-start.1 = ((f32[8,128,224]{1,2,0:T(8,128)}), f32[8,128,224]{1,2,0:T(8,128)S(1)}, u32[]{:S(2)}, u32[]{:S(2)}) async-start(f32[8,128,224]{1,2,0:T(8,128)} %convolution_bitcast_fusion.3), calls=%async_computation.1 | async-start | bytes 1835008 | tf_op jit(solution)/shard_map/while/body/eval_jaxpr/all_to_all | solution.py:44
  236.8 15.3 %copy-start.2 = (bf16[512,1792]{1,0:T(8,128)(2,1)S(1)}, bf16[512,1792]{1,0:T(8,128)(2,1)}, u32[]{:S(2)}) copy-start(bf16[512,1792]{1,0:T(8,128)(2,1)} %get-tuple-element.397) | copy-start | bytes 5505028 | tf_op jit(solution)/shard_map/while
  253.7 15.7 %all-to-all-start.2 = ((f32[8,64,128]{2,1,0:T(8,128)}), f32[8,64,128]{2,1,0:T(8,128)S(1)}, u32[]{:S(2)}, u32[]{:S(2)}) async-start(f32[8,64,128]{2,1,0:T(8,128)} %bitcast.122), calls=%async_computation.2 | async-start | bytes 524288 | tf_op jit(solution)/shard_map/while/body/eval_jaxpr/all_to_all | solution.py:44
  270.1 13.8 %all-to-all-start.3 = ((f32[64,1,128]{2,1,0:T(1,128)}), f32[64,1,128]{2,1,0:T(1,128)S(1)}, u32[]{:S(2)}, u32[]{:S(2)}) async-start(f32[64,1,128]{2,1,0:T(1,128)} %broadcast_in_dim.64), calls=%async_computation.3 | async-start | bytes 65536 | tf_op jit(solution)/shard_map/while/body/eval_jaxpr/all_to_all | solution.py:19
  284.0 4.3 collective-permute-start
  301.8 19.9 %all-to-all-start.1 = ((f32[8,128,224]{1,2,0:T(8,128)}), f32[8,128,224]{1,2,0:T(8,128)S(1)}, u32[]{:S(2)}, u32[]{:S(2)}) async-start(f32[8,128,224]{1,2,0:T(8,128)} %convolution_bitcast_fusion.3), calls=%async_computation.1 | async-start | bytes 1835008 | tf_op jit(solution)/shard_map/while/body/eval_jaxpr/all_to_all | solution.py:44
  322.7 15.3 %copy-start.2 = (bf16[512,1792]{1,0:T(8,128)(2,1)S(1)}, bf16[512,1792]{1,0:T(8,128)(2,1)}, u32[]{:S(2)}) copy-start(bf16[512,1792]{1,0:T(8,128)(2,1)} %get-tuple-element.397) | copy-start | bytes 5505028 | tf_op jit(solution)/shard_map/while
  339.5 15.7 %all-to-all-start.2 = ((f32[8,64,128]{2,1,0:T(8,128)}), f32[8,64,128]{2,1,0:T(8,128)S(1)}, u32[]{:S(2)}, u32[]{:S(2)}) async-start(f32[8,64,128]{2,1,0:T(8,128)} %bitcast.122), calls=%async_computation.2 | async-start | bytes 524288 | tf_op jit(solution)/shard_map/while/body/eval_jaxpr/all_to_all | solution.py:44
  356.0 13.8 %all-to-all-start.3 = ((f32[64,1,128]{2,1,0:T(1,128)}), f32[64,1,128]{2,1,0:T(1,128)S(1)}, u32[]{:S(2)}, u32[]{:S(2)}) async-start(f32[64,1,128]{2,1,0:T(1,128)} %broadcast_in_dim.64), calls=%async_computation.3 | async-start | bytes 65536 | tf_op jit(solution)/shard_map/while/body/eval_jaxpr/all_to_all | solution.py:19
  369.9 4.3 collective-permute-start
  387.7 19.9 %all-to-all-start.1 = ((f32[8,128,224]{1,2,0:T(8,128)}), f32[8,128,224]{1,2,0:T(8,128)S(1)}, u32[]{:S(2)}, u32[]{:S(2)}) async-start(f32[8,128,224]{1,2,0:T(8,128)} %convolution_bitcast_fusion.3), calls=%async_computation.1 | async-start | bytes 1835008 | tf_op jit(solution)/shard_map/while/body/eval_jaxpr/all_to_all | solution.py:44
  408.5 15.3 %copy-start.2 = (bf16[512,1792]{1,0:T(8,128)(2,1)S(1)}, bf16[512,1792]{1,0:T(8,128)(2,1)}, u32[]{:S(2)}) copy-start(bf16[512,1792]{1,0:T(8,128)(2,1)} %get-tuple-element.397) | copy-start | bytes 5505028 | tf_op jit(solution)/shard_map/while
  425.4 15.7 %all-to-all-start.2 = ((f32[8,64,128]{2,1,0:T(8,128)}), f32[8,64,128]{2,1,0:T(8,128)S(1)}, u32[]{:S(2)}, u32[]{:S(2)}) async-start(f32[8,64,128]{2,1,0:T(8,128)} %bitcast.122), calls=%async_computation.2 | async-start | bytes 524288 | tf_op jit(solution)/shard_map/while/body/eval_jaxpr/all_to_all | solution.py:44
  441.9 13.8 %all-to-all-start.3 = ((f32[64,1,128]{2,1,0:T(1,128)}), f32[64,1,128]{2,1,0:T(1,128)S(1)}, u32[]{:S(2)}, u32[]{:S(2)}) async-start(f32[64,1,128]{2,1,0:T(1,128)} %broadcast_in_dim.64), calls=%async_computation.3 | async-start | bytes 65536 | tf_op jit(solution)/shard_map/while/body/eval_jaxpr/all_to_all | solution.py:19
  455.8 4.3 collective-permute-start
  473.5 19.9 %all-to-all-start.1 = ((f32[8,128,224]{1,2,0:T(8,128)}), f32[8,128,224]{1,2,0:T(8,128)S(1)}, u32[]{:S(2)}, u32[]{:S(2)}) async-start(f32[8,128,224]{1,2,0:T(8,128)} %convolution_bitcast_fusion.3), calls=%async_computation.1 | async-start | bytes 1835008 | tf_op jit(solution)/shard_map/while/body/eval_jaxpr/all_to_all | solution.py:44
  494.4 15.3 %copy-start.2 = (bf16[512,1792]{1,0:T(8,128)(2,1)S(1)}, bf16[512,1792]{1,0:T(8,128)(2,1)}, u32[]{:S(2)}) copy-start(bf16[512,1792]{1,0:T(8,128)(2,1)} %get-tuple-element.397) | copy-start | bytes 5505028 | tf_op jit(solution)/shard_map/while
  511.3 15.7 %all-to-all-start.2 = ((f32[8,64,128]{2,1,0:T(8,128)}), f32[8,64,128]{2,1,0:T(8,128)S(1)}, u32[]{:S(2)}, u32[]{:S(2)}) async-start(f32[8,64,128]{2,1,0:T(8,128)} %bitcast.122), calls=%async_computation.2 | async-start | bytes 524288 | tf_op jit(solution)/shard_map/while/body/eval_jaxpr/all_to_all | solution.py:44
  527.8 13.8 %all-to-all-start.3 = ((f32[64,1,128]{2,1,0:T(1,128)}), f32[64,1,128]{2,1,0:T(1,128)S(1)}, u32[]{:S(2)}, u32[]{:S(2)}) async-start(f32[64,1,128]{2,1,0:T(1,128)} %broadcast_in_dim.64), calls=%async_computation.3 | async-start | bytes 65536 | tf_op jit(solution)/shard_map/while/body/eval_jaxpr/all_to_all | solution.py:19
  541.7 4.3 collective-permute-start
  559.4 19.9 %all-to-all-start.1 = ((f32[8,128,224]{1,2,0:T(8,128)}), f32[8,128,224]{1,2,0:T(8,128)S(1)}, u32[]{:S(2)}, u32[]{:S(2)}) async-start(f32[8,128,224]{1,2,0:T(8,128)} %convolution_bitcast_fusion.3), calls=%async_computation.1 | async-start | bytes 1835008 | tf_op jit(solution)/shard_map/while/body/eval_jaxpr/all_to_all | solution.py:44
  580.3 15.3 %copy-start.2 = (bf16[512,1792]{1,0:T(8,128)(2,1)S(1)}, bf16[512,1792]{1,0:T(8,128)(2,1)}, u32[]{:S(2)}) copy-start(bf16[512,1792]{1,0:T(8,128)(2,1)} %get-tuple-element.397) | copy-start | bytes 5505028 | tf_op jit(solution)/shard_map/while
  597.2 15.7 %all-to-all-start.2 = ((f32[8,64,128]{2,1,0:T(8,128)}), f32[8,64,128]{2,1,0:T(8,128)S(1)}, u32[]{:S(2)}, u32[]{:S(2)}) async-start(f32[8,64,128]{2,1,0:T(8,128)} %bitcast.122), calls=%async_computation.2 | async-start | bytes 524288 | tf_op jit(solution)/shard_map/while/body/eval_jaxpr/all_to_all | solution.py:44
  613.7 13.8 %all-to-all-start.3 = ((f32[64,1,128]{2,1,0:T(1,128)}), f32[64,1,128]{2,1,0:T(1,128)S(1)}, u32[]{:S(2)}, u32[]{:S(2)}) async-start(f32[64,1,128]{2,1,0:T(1,128)} %broadcast_in_dim.64), calls=%async_computation.3 | async-start | bytes 65536 | tf_op jit(solution)/shard_map/while/body/eval_jaxpr/all_to_all | solution.py:19
  627.6 4.3 collective-permute-start.1
  631.9 16.5 %copy-start.5 = (f32[128,64]{0,1:T(8,128)}, f32[128,64]{0,1:T(8,128)S(1)}, u32[]{:S(2)}) copy-start(f32[128,64]{0,1:T(8,128)S(1)} %fusion.25) | copy-start | bytes 98308
where the time goes:
time: 651 us; the launch traced here: 648 us
  waiting for transfers between devices  257 us (39%)
  blocking collectives  189 us (29%)
  starting transfers between devices  139 us (21%)
  matrix products  33.2 us (5%)
  local copies, waits for them, and re-layouts  18 us (3%)
  other arithmetic  10.4 us (2%)
    all_to_all x14, waiting for transfers between devices, summed_on_arrival(): lax.all_to_all(tiles, axis, split_axis=0, concat_axis=0, tiled=True)  181 us
    all_gather x7, blocking collectives, rows_first(): out = lax.all_gather(both, axis, axis=0, tiled=True)  102 us
    all_to_all x8, blocking collectives, sent_to_all(): lax.all_to_all(jnp.broadcast_to(x[None], (devices, *x.shape)), axis, 0, 0...  87.4 us
    all_to_all x14, starting transfers between devices, summed_on_arrival(): lax.all_to_all(tiles, axis, split_axis=0, concat_axis=0, tiled=True)  68.6 us
    all_to_all x8, waiting for transfers between devices, sent_to_all(): lax.all_to_all(jnp.broadcast_to(x[None], (devices, *x.shape)), axis, 0, 0...  67.6 us
    all_to_all x8, starting transfers between devices, sent_to_all(): lax.all_to_all(jnp.broadcast_to(x[None], (devices, *x.shape)), axis, 0, 0...  44.7 us
    ppermute x8, starting transfers between devices, shifted(): lax.ppermute(x, axis, [(i, (i + by) % devices) for i in range(devices)])  26.1 us
    dot_general x7, matrix products, layer_step(): lax.dot_general(wide, wd, (((1,), (1,)), ((), ())), preferred_element_typ...  21.4 us
  transfers between devices with their start and end apart: 30, of which 30 were waited for; matrix products, arithmetic and copies ran while one was open for 1% of the time, Pallas kernels for 0%

commit v1 on v0

v1 whole, which is shorter than its diff:
```python
import jax
import jax.numpy as jnp
from jax import lax
from jax.experimental import pallas as pl
from jax.experimental.pallas import tpu as pltpu
from jax.sharding import PartitionSpec as P

D = 4096
FF = 14336
ROWS = 128
UPD = 8
MB = 4
SECTIONS, ROW, COL = 4, 8, 8
XS = ROW // 2
CHUNK = D // (ROW * COL)
FEATS = D // ROW
HID = FF // COL
HALF = HID // 2
PIECE = HID // ROW
FAR_Z = (4, 3, 5, 2, 6, 1, 7)
FAR_X = (2, 1, 3)
SLOTS = MB + 3

eps = 1e-05
bf16 = jnp.bfloat16
f32 = jnp.float32
MESH = pl.DeviceIdType.MESH


def kernel(
    cot_h, inc_h, u_h, v_h, x_h, h_h, gain_h, wg_h, wu_h, wd_h,
    new_o, res_o,
    cot_v, inc_v, u_v, v_v, x_v, h_v, gain_v, wg_v, wu_v, wd_v,
    cot_t, inc_t, u_t, v_t, x_t, gain_t, gx, slope,
    start, gy, gys, carry, after, d1s, d1r, own, xsd, xrv, mine, ga, grads, acc, zs, zr,
    ixs, ixr, izs, izr, sqs, sqz, sqm, sqx, rstd, home, dxs, dxr, dzs, dzr,
    load, first, ss, rs, one_s, one_r,
):
    s = lax.axis_index("section")
    r = lax.axis_index("row")
    c = lax.axis_index("col")
    core = lax.rem(r, 2)
    x = lax.div(r, 2)
    mate = r + 1 - 2 * core

    def at_col(k):
        return lax.rem(c + k, COL)

    def at_x(k):
        return lax.rem(x + k, XS)

    def remote(src, dst, send, recv, device):
        return pltpu.make_async_remote_copy(
            src_ref=src, dst_ref=dst, send_sem=send, recv_sem=recv, device_id=device, device_id_type=MESH
        )

    def arrived(ref, recv):
        remote(ref, ref, one_s.at[0], recv, (s, mate, c)).wait_recv()

    def left(ref, send):
        remote(ref, ref, send, one_r.at[0], (s, mate, c)).wait_send()

    loads = {}
    for i, (name, src, dst) in enumerate(
        (
            ("cot", cot_h.at[0], cot_v),
            ("gain", gain_h, gain_v),
            ("x", x_h.at[0], x_v),
            ("wd", wd_h.at[0], wd_v),
            ("h", h_h.at[0], h_v),
            ("wg0", wg_h.at[0, :, pl.ds(0, HALF)], wg_v.at[0]),
            ("wg1", wg_h.at[0, :, pl.ds(HALF, HALF)], wg_v.at[1]),
            ("wu0", wu_h.at[0, :, pl.ds(0, HALF)], wu_v.at[0]),
            ("wu1", wu_h.at[0, :, pl.ds(HALF, HALF)], wu_v.at[1]),
            ("inc", inc_h.at[0], inc_v),
            ("u", u_h.at[0], u_v),
            ("v", v_h.at[0], v_v),
        )
    ):
        loads[name] = pltpu.make_async_copy(src, dst, load.at[i])
        loads[name].start()

    barrier = pltpu.get_barrier_semaphore()
    for ds in range(SECTIONS):
        for dc in range(COL):
            if ds or dc:
                there = (lax.rem(s + ds, SECTIONS), r, at_col(dc))
                pl.semaphore_signal(barrier, inc=1, device_id=there, device_id_type=MESH)
    for dr in range(1, ROW):
        pl.semaphore_signal(barrier, inc=1, device_id=(s, lax.rem(r + dr, ROW), c), device_id_type=MESH)

    loads["cot"].wait()
    cot_t[...] = cot_v[...].T
    start[...] = cot_t[...].astype(bf16)
    pl.semaphore_wait(barrier, SECTIONS * COL - 1 + ROW - 1)

    LAST = SECTIONS - 1
    mb_home = s

    @pl.when(s == LAST)
    def _():
        gy[LAST, c] = start[...]
        carry[LAST] = cot_t[...]
        for k in FAR_Z:
            remote(start, gy.at[LAST, c], first.at[0], rs.at[0, LAST], (LAST, r, at_col(k))).start()

    @pl.when(s != LAST)
    def _():
        for k in (*FAR_Z, 0):
            remote(start, gy.at[mb_home, c], first.at[0], rs.at[0, mb_home], (LAST, r, at_col(k))).start()
        remote(cot_t, carry.at[mb_home], first.at[1], rs.at[1, mb_home], (LAST, r, c)).start()

    loads["gain"].wait()
    loads["x"].wait()
    gain_t[...] = jnp.broadcast_to(gain_v[...], (ROWS, CHUNK)).T
    sums = []
    for m in range(MB):
        xt = x_v[m].astype(f32).T
        x_t[m] = xt
        gx[c, m] = (gain_t[...] * xt).astype(bf16)
        sums.append(jnp.sum(xt * xt, axis=0, keepdims=True))
    sums = jnp.concatenate(sums + sums, axis=0)
    sqs[...] = sums
    sqz[c] = sums
    for k in FAR_Z:
        remote(gx.at[c], gx.at[c], one_s.at[1], one_r.at[1], (s, r, at_col(k))).start()
        remote(sqs, sqz.at[c], one_s.at[2], one_r.at[2], (s, r, at_col(k))).start()

    def slopes(m):
        for half in range(2):
            for b in range(7):
                at = pl.ds(half * HALF + b * 128, 128)
                hg = h_v[m, 0, :, at].astype(f32)
                hu = h_v[m, 1, :, at].astype(f32)
                sig = jax.nn.sigmoid(hg)
                slope[m, 0, half, pl.ds(b * 128, 128)] = (hu * sig * (1.0 + hg * (1.0 - sig))).T
                slope[m, 1, half, pl.ds(b * 128, 128)] = (hg * sig).T

    def epilogue_inputs():
        inc_t[...] = inc_v[...].T
        for i in range(UPD):
            u_t[i] = u_v[i].T
            v_t[i] = v_v[i].T

    loads["h"].wait()
    loads["inc"].wait()
    loads["u"].wait()
    loads["v"].wait()

    @pl.when(s != LAST)
    def _():
        epilogue_inputs()

        def body(m, carry_):
            slopes(m)
            return carry_

        lax.fori_loop(0, MB, body, 0)

    @pl.when(s == LAST)
    def _():
        slopes(LAST)

    for name in ("wd", "wg0", "wg1", "wu0", "wu1"):
        loads[name].wait()

    def hidden(m):
        @pl.when(jnp.logical_and(s == LAST, m == LAST))
        def _():
            arrived(gy.at[m, pl.ds(0, COL - 1)], rs.at[0, m])

        @pl.when(jnp.logical_not(jnp.logical_and(s == LAST, m == LAST)))
        def _():
            arrived(gy.at[m], rs.at[0, m])
            arrived(carry.at[m], rs.at[1, m])

        g = gy[m].reshape(FEATS, ROWS)
        for i in range(XS):
            d1s[m, i] = jnp.dot(wd_v[(1 - core) * XS + i], g, preferred_element_type=f32).astype(bf16)
        remote(d1s.at[m], d1r.at[m], ss.at[2, m], rs.at[2, m], (s, mate, c)).start()
        for i in range(XS):
            own[m, i] = jnp.dot(wd_v[core * XS + i], g, preferred_element_type=f32)

    def halved(m):
        arrived(d1r.at[m], rs.at[2, m])
        for k in FAR_X:
            to = at_x(k)
            xsd[m, to] = (own[m, to] + d1r[m, to].astype(f32)).astype(bf16)
            remote(xsd.at[m, to], xrv.at[m, x], ss.at[3, m], rs.at[3, m], (s, 2 * to + core, c)).start()
        mine[m] = own[m, x] + d1r[m, x].astype(f32)

    def summed(m):
        arrived(xrv.at[m, pl.ds(0, XS - 1)], rs.at[3, m])
        total = mine[m]
        for k in FAR_X:
            total = total + xrv[m, at_x(k)].astype(f32)
        ga[m, core, x] = total.astype(bf16)
        for k in FAR_X:
            remote(ga.at[m, core, x], ga.at[m, core, x], ss.at[4, m], rs.at[4, m], (s, 2 * at_x(k) + core, c)).start()

    def gradients(m, half):
        g = ga[m, half].reshape(HALF, ROWS).astype(f32)
        grads[0] = (g * slope[m, 0, half]).astype(bf16)
        grads[1] = (g * slope[m, 1, half]).astype(bf16)

    def spread(m):
        arrived(ga.at[m, core, pl.ds(0, XS - 1)], rs.at[4, m])
        remote(ga.at[m, core], ga.at[m, core], ss.at[5, m], rs.at[5, m], (s, mate, c)).start()
        gradients(m, core)
        for b in range(2):
            rows = pl.ds(b * 256, 256)
            acc[rows] = jnp.dot(wg_v[core, rows], grads[0], preferred_element_type=f32) + jnp.dot(
                wu_v[core, rows], grads[1], preferred_element_type=f32
            )

    def features(m):
        other = 1 - core
        arrived(ga.at[m, other], rs.at[5, m])
        gradients(m, other)
        inner = jnp.zeros((1, ROWS), f32)
        for b in range(2):
            rows = pl.ds(b * 256, 256)
            part = (
                acc[rows]
                + jnp.dot(wg_v[other, rows], grads[0], preferred_element_type=f32)
                + jnp.dot(wu_v[other, rows], grads[1], preferred_element_type=f32)
            )
            scaled = gx[pl.ds(4 * b, 4), m].reshape(256, ROWS).astype(f32)
            inner = inner + jnp.sum(part * scaled, axis=0, keepdims=True)
            zs[m, pl.ds(4 * b, 4)] = part.astype(bf16).reshape(4, CHUNK, ROWS)
        for k in FAR_Z:
            to = at_col(k)
            remote(zs.at[m, to], zr.at[m, c], ss.at[6, m], rs.at[6, m], (s, r, to)).start()
        zr[m, c] = zs[m, c]
        ixs[m] = inner
        ixr[m, r] = inner
        for k in range(1, ROW):
            remote(ixs.at[m], ixr.at[m, r], ss.at[7, m], rs.at[7, m], (s, lax.rem(r + k, ROW), c)).start()

    def projected(m):
        arrived(ixr.at[m, pl.ds(0, ROW - 1)], rs.at[7, m])
        inner = jnp.sum(ixr[m], axis=0)
        izs[m] = inner
        izr[m, c] = inner
        for k in FAR_Z:
            remote(izs.at[m], izr.at[m, c], ss.at[8, m], rs.at[8, m], (s, r, at_col(k))).start()

    def updated(m):
        arrived(zr.at[m, pl.ds(0, COL - 1)], rs.at[6, m])
        arrived(izr.at[m, pl.ds(0, COL - 1)], rs.at[8, m])
        total = jnp.sum(zr[m].astype(f32), axis=0)
        inner = jnp.sum(izr[m], axis=0) / D
        root = rstd[m]
        fresh = carry[m] + root * (gain_t[...] * total) - x_t[m] * (root * root * root) * inner
        after[m] = fresh

        @pl.when(s != 0)
        def _():
            gys[m] = fresh.astype(bf16)
            for k in (*FAR_Z, 0):
                remote(gys.at[m], gy.at[m, c], ss.at[0, m], rs.at[0, m], (s - 1, r, at_col(k))).start()
            remote(after.at[m], carry.at[m], ss.at[1, m], rs.at[1, m], (s - 1, r, c)).start()

        @pl.when(jnp.logical_and(s == 0, m != 0))
        def _():
            remote(after.at[m], home, ss.at[1, m], one_r.at[4], (m, r, c)).start()

        @pl.when(jnp.logical_and(s == 0, m == 0))
        def _():
            home[...] = fresh

    def squares_met():
        arrived(sqz.at[pl.ds(0, COL - 1)], one_r.at[2])
        total = jnp.sum(sqz[...], axis=0)
        sqm[...] = total
        sqx[r] = total
        for k in range(1, ROW):
            remote(sqm, sqx.at[r], one_s.at[3], one_r.at[3], (s, lax.rem(r + k, ROW), c)).start()

    def roots():
        arrived(sqx.at[pl.ds(0, ROW - 1)], one_r.at[3])
        arrived(gx.at[pl.ds(0, COL - 1)], one_r.at[1])
        root = lax.rsqrt(jnp.sum(sqx[...], axis=0) / D + eps)
        for m in range(MB):
            rstd[m] = root[m : m + 1]

    def slot(t, carry_):
        def stage(lag, body):
            @pl.when(jnp.logical_and(t >= lag, t < lag + MB))
            def _():
                body(LAST - (t - lag))

        stage(0, hidden)

        @pl.when(t == 0)
        def _():
            squares_met()

        stage(2, spread)
        stage(1, summed)
        stage(0, halved)

        @pl.when(jnp.logical_and(s == LAST, t < LAST))
        def _():
            slopes(LAST - 1 - t)

        @pl.when(t == 1)
        def _():
            roots()

        stage(2, features)
        stage(3, updated)
        stage(2, projected)
        return carry_

    lax.fori_loop(0, SLOTS, slot, 0)

    @pl.when(s == LAST)
    def _():
        epilogue_inputs()

    @pl.when(s != 0)
    def _():
        arrived(home, one_r.at[4])

    resid = home[...] + inc_t[...] - cot_t[...]
    res_o[...] = resid
    part = jnp.concatenate([jnp.sum(v_t[i] * resid, axis=0, keepdims=True) for i in range(UPD)], axis=0)
    dxs[...] = part
    dxr[r] = part
    for k in range(1, ROW):
        remote(dxs, dxr.at[r], one_s.at[5], one_r.at[5], (s, lax.rem(r + k, ROW), c)).start()
    arrived(dxr.at[pl.ds(0, ROW - 1)], one_r.at[5])
    part = jnp.sum(dxr[...], axis=0)
    dzs[...] = part
    dzr[c] = part
    for k in FAR_Z:
        remote(dzs, dzr.at[c], one_s.at[6], one_r.at[6], (s, r, at_col(k))).start()
    arrived(dzr.at[pl.ds(0, COL - 1)], one_r.at[6])
    dots = jnp.sum(jnp.sum(dzr[...], axis=0), axis=1, keepdims=True)
    update = dots[0:1] * u_t[0]
    for i in range(1, UPD):
        update = update + dots[i : i + 1] * u_t[i]
    new_o[...] = cot_t[...] + resid - update

    @pl.when(s == LAST)
    def _():
        left(gy.at[0, pl.ds(0, COL - 1)], first.at[0])

    @pl.when(s != LAST)
    def _():
        left(gy.at[0], first.at[0])
        left(cot_t, first.at[1])

    left(gx.at[pl.ds(0, COL - 1)], one_s.at[1])
    left(sqz.at[pl.ds(0, COL - 1)], one_s.at[2])
    left(sqx.at[pl.ds(0, ROW - 1)], one_s.at[3])
    left(dxr.at[pl.ds(0, ROW - 1)], one_s.at[5])
    left(dzr.at[pl.ds(0, COL - 1)], one_s.at[6])

    def drained(m, carry_):
        @pl.when(s != 0)
        def _():
            left(gy.at[m], ss.at[0, m])

        @pl.when(jnp.logical_or(s != 0, m != 0))
        def _():
            left(after.at[m], ss.at[1, m])

        left(d1s.at[m], ss.at[2, m])
        left(xrv.at[m, pl.ds(0, XS - 1)], ss.at[3, m])
        left(ga.at[m, core, pl.ds(0, XS - 1)], ss.at[4, m])
        left(ga.at[m, core], ss.at[5, m])
        left(zr.at[m, pl.ds(0, COL - 1)], ss.at[6, m])
        left(ixr.at[m, pl.ds(0, ROW - 1)], ss.at[7, m])
        left(izr.at[m, pl.ds(0, COL - 1)], ss.at[8, m])
        return carry_

    lax.fori_loop(0, MB, drained, 0)


def shards(cotangent, incoming, upd_u, upd_v, saved_x, saved_h, norm_gain, w_gate, w_up, w_down):
    vm = pltpu.VMEM
    dma = pltpu.SemaphoreType.DMA
    tile = (CHUNK, ROWS)
    new, res = pl.pallas_call(
        kernel,
        out_shape=[jax.ShapeDtypeStruct(tile, f32)] * 2,
        in_specs=[pl.BlockSpec(memory_space=pl.ANY)] * 10,
        out_specs=[pl.BlockSpec(memory_space=pltpu.VMEM)] * 2,
        scratch_shapes=[
            vm((ROWS, CHUNK), f32),
            vm((ROWS, CHUNK), f32),
            vm((UPD, ROWS, CHUNK), f32),
            vm((UPD, ROWS, CHUNK), f32),
            vm((MB, ROWS, CHUNK), bf16),
            vm((MB, 2, ROWS, HID), bf16),
            vm((1, CHUNK), f32),
            vm((2, FEATS, HALF), bf16),
            vm((2, FEATS, HALF), bf16),
            vm((ROW, PIECE, FEATS), bf16),
            vm(tile, f32),
            vm(tile, f32),
            vm((UPD, *tile), f32),
            vm((UPD, *tile), f32),
            vm((MB, *tile), f32),
            vm(tile, f32),
            vm((COL, MB, *tile), bf16),
            vm((MB, 2, 2, HALF, ROWS), f32),
            vm(tile, bf16),
            vm((MB, COL, *tile), bf16),
            vm((MB, *tile), bf16),
            vm((MB, *tile), f32),
            vm((MB, *tile), f32),
            vm((MB, XS, PIECE, ROWS), bf16),
            vm((MB, XS, PIECE, ROWS), bf16),
            vm((MB, XS, PIECE, ROWS), f32),
            vm((MB, XS, PIECE, ROWS), bf16),
            vm((MB, XS, PIECE, ROWS), bf16),
            vm((MB, PIECE, ROWS), f32),
            vm((MB, 2, XS, PIECE, ROWS), bf16),
            vm((2, HALF, ROWS), bf16),
            vm((FEATS, ROWS), f32),
            vm((MB, COL, *tile), bf16),
            vm((MB, COL, *tile), bf16),
            vm((MB, 1, ROWS), f32),
            vm((MB, ROW, 1, ROWS), f32),
            vm((MB, 1, ROWS), f32),
            vm((MB, COL, 1, ROWS), f32),
            vm((8, ROWS), f32),
            vm((COL, 8, ROWS), f32),
            vm((8, ROWS), f32),
            vm((ROW, 8, ROWS), f32),
            vm((MB, 1, ROWS), f32),
            vm(tile, f32),
            vm((UPD, ROWS), f32),
            vm((ROW, UPD, ROWS), f32),
            vm((UPD, ROWS), f32),
            vm((COL, UPD, ROWS), f32),
            dma((12,)),
            dma((2,)),
            dma((9, MB)),
            dma((9, MB)),
            dma((7,)),
            dma((7,)),
        ],
        compiler_params=pltpu.CompilerParams(
            collective_id=0, has_side_effects=True, vmem_limit_bytes=60 * 1024 * 1024
        ),
        name="broyden",
    )(
        cotangent, incoming, upd_u, upd_v, saved_x, saved_h, norm_gain,
        w_gate, w_up, w_down.reshape(1, ROW, PIECE, FEATS),
    )
    return new.T[None], res.T[None]


def solution(mesh):
    placed = (
        P("section", None, ("row", "col")),
        P("section", None, ("row", "col")),
        P("section", None, None, ("row", "col")),
        P("section", None, None, ("row", "col")),
        P("section", None, None, ("row", "col")),
        P("section", None, None, None, "col"),
        P("section", ("row", "col")),
        P("section", "row", "col"),
        P("section", "row", "col"),
        P("section", "col", "row"),
    )
    return jax.shard_map(
        shards,
        mesh=mesh,
        in_specs=placed,
        out_specs=(P("section", None, ("row", "col")), P("section", None, ("row", "col"))),
        check_vma=False,
    )
```

time: 651 us -> 197 us (0.30)
  waiting for transfers between devices: 257 us -> 0 us
  blocking collectives: 189 us -> 0 us
  Pallas kernels: 0 us -> 185 us
  starting transfers between devices: 139 us -> 0 us
  matrix products: 33.2 us -> 0 us
  other arithmetic: 10.4 us -> 0 us
  local copies, waits for them, and re-layouts: 18 us -> 11.2 us
    all_to_all x22 -> x0, waiting for transfers between devices: 249 us -> none  [the longest x14 181 us: summed_on_arrival(): lax.all_to_all(tiles, axis, split_axis=0, concat_axis=0, tiled=True)]
    pallas_call x0 -> x1, Pallas kernels: none -> 185 us  [shards(): pl.pallas_call(kernel, out_shape=[jax.ShapeDtypeStruct(tile, f32)] * 2, i...]
    all_to_all x22 -> x0, starting transfers between devices: 113 us -> none  [the longest x14 68.6 us: summed_on_arrival(): lax.all_to_all(tiles, axis, split_axis=0, concat_axis=0, tiled=True)]
    all_gather x7 -> x0, blocking collectives: 102 us -> none  [rows_first(): out = lax.all_gather(both, axis, axis=0, tiled=True)]
    all_to_all x8 -> x0, blocking collectives: 87.4 us -> none  [sent_to_all(): lax.all_to_all(jnp.broadcast_to(x[None], (devices, *x.shape)), axis, 0, 0...]
    dot_general x23 -> x0, matrix products: 33.2 us -> none  [the longest x7 21.4 us: layer_step(): lax.dot_general(wide, wd, (((1,), (1,)), ((), ())), preferred_element_typ...]
    ppermute x8 -> x0, starting transfers between devices: 26.1 us -> none  [shifted(): lax.ppermute(x, axis, [(i, (i + by) % devices) for i in range(devices)])]
    ppermute x8 -> x0, waiting for transfers between devices: 8.19 us -> none  [shifted(): lax.ppermute(x, axis, [(i, (i + by) % devices) for i in range(devices)])]
  transfers between devices with their start and end apart: 30 -> 0, of which waited for: 30 -> 0; matrix products, arithmetic and copies ran while one was open for 1% -> 0% of each run, Pallas kernels for 0% -> 0%
where the time goes in v1:
time: 197 us; the launch traced here: 196 us
  Pallas kernels  185 us (94%)
  local copies, waits for them, and re-layouts  11.2 us (6%)
    pallas_call x1, Pallas kernels, shards(): pl.pallas_call(kernel, out_shape=[jax.ShapeDtypeStruct(tile, f32)] * 2, i...  185 us
    unnamed x7, local copies, waits for them, and re-layouts  11.2 us

profile of v1, /device:TPU:1, one launch (start us, length us, event | category | flops | bytes accessed | tf_op | source)
XLA Modules:
  0.0 196.4 jit_solution(6916120245187907466)
XLA Ops:
  0.6 1.5 copy.12.cot_h
  2.1 1.5 copy.13.inc_h
  3.6 1.6 copy.16.x_h
  5.2 1.9 copy.14.u_h
  7.1 2.0 copy.15.v_h
  9.1 184.6 %broyden.1 = (f32[64,128]{1,0:T(8,128)}, f32[64,128]{1,0:T(8,128)}) custom-call(f32[1,128,64]{2,1,0:T(8,128)} %copy.12.cot_h, f32[1,128,64]{2,1,0:T(8,128)} %copy.13.inc_h, f32[1,8,128,64]{3,2,1,0:T(8,128)} %copy.14.u_h, f32[1,8,128,64]{3,2,1,0:T(8,128)} %copy.15.v_h, bf16[1,4,128,64]{3,2,1,0:T(8,128)(2,1)} %copy.16.x_h, bf16[1,4,2,128,1792]{4,3,2,1,0:T(8,128)(2,1)} %h_h.1, ...), custom_call_target="tpu_custom_call" | custom-call | tf_op jit(solution)/shard_map/broyden/pallas_call | solution.py:386
  193.7 1.4 copy.19
  195.0 1.4 copy.20

commit v2 on v1

--- a/solution.py
+++ b/solution.py
@@ -30,8 +30,8 @@
 def kernel(
     cot_h, inc_h, u_h, v_h, x_h, h_h, gain_h, wg_h, wu_h, wd_h,
     new_o, res_o,
-    cot_v, inc_v, u_v, v_v, x_v, h_v, gain_v, wg_v, wu_v, wd_v,
-    cot_t, inc_t, u_t, v_t, x_t, gain_t, gx, slope,
+    cot_t, inc_t, u_t, v_t, x_v, h_v, gain_v, wg_v, wu_v, wd_v,
+    x_t, gain_t, gx, slope,
     start, gy, gys, carry, after, d1s, d1r, own, xsd, xrv, mine, ga, grads, acc, zs, zr,
     ixs, ixr, izs, izr, sqs, sqz, sqm, sqx, rstd, home, dxs, dxr, dzs, dzr,
     load, first, ss, rs, one_s, one_r,
@@ -63,7 +63,7 @@
     loads = {}
     for i, (name, src, dst) in enumerate(
         (
-            ("cot", cot_h.at[0], cot_v),
+            ("cot", cot_h.at[0], cot_t),
             ("gain", gain_h, gain_v),
             ("x", x_h.at[0], x_v),
             ("wd", wd_h.at[0], wd_v),
@@ -72,9 +72,9 @@
             ("wg1", wg_h.at[0, :, pl.ds(HALF, HALF)], wg_v.at[1]),
             ("wu0", wu_h.at[0, :, pl.ds(0, HALF)], wu_v.at[0]),
             ("wu1", wu_h.at[0, :, pl.ds(HALF, HALF)], wu_v.at[1]),
-            ("inc", inc_h.at[0], inc_v),
-            ("u", u_h.at[0], u_v),
-            ("v", v_h.at[0], v_v),
+            ("inc", inc_h.at[0], inc_t),
+            ("u", u_h.at[0], u_t),
+            ("v", v_h.at[0], v_t),
         )
     ):
         loads[name] = pltpu.make_async_copy(src, dst, load.at[i])
@@ -90,7 +90,6 @@
         pl.semaphore_signal(barrier, inc=1, device_id=(s, lax.rem(r + dr, ROW), c), device_id_type=MESH)
 
     loads["cot"].wait()
-    cot_t[...] = cot_v[...].T
     start[...] = cot_t[...].astype(bf16)
     pl.semaphore_wait(barrier, SECTIONS * COL - 1 + ROW - 1)
 
@@ -115,7 +114,7 @@
     gain_t[...] = jnp.broadcast_to(gain_v[...], (ROWS, CHUNK)).T
     sums = []
     for m in range(MB):
-        xt = x_v[m].astype(f32).T
+        xt = x_v[m].astype(f32)
         x_t[m] = xt
         gx[c, m] = (gain_t[...] * xt).astype(bf16)
         sums.append(jnp.sum(xt * xt, axis=0, keepdims=True))
@@ -136,12 +135,6 @@
                 slope[m, 0, half, pl.ds(b * 128, 128)] = (hu * sig * (1.0 + hg * (1.0 - sig))).T
                 slope[m, 1, half, pl.ds(b * 128, 128)] = (hg * sig).T
 
-    def epilogue_inputs():
-        inc_t[...] = inc_v[...].T
-        for i in range(UPD):
-            u_t[i] = u_v[i].T
-            v_t[i] = v_v[i].T
-
     loads["h"].wait()
     loads["inc"].wait()
     loads["u"].wait()
@@ -149,8 +142,6 @@
 
     @pl.when(s != LAST)
     def _():
-        epilogue_inputs()
-
         def body(m, carry_):
             slopes(m)
             return carry_
@@ -315,10 +306,6 @@
 
     lax.fori_loop(0, SLOTS, slot, 0)
 
-    @pl.when(s == LAST)
-    def _():
-        epilogue_inputs()
-
     @pl.when(s != 0)
     def _():
         arrived(home, one_r.at[4])
@@ -379,6 +366,10 @@
     lax.fori_loop(0, MB, drained, 0)
 
 
+def turned(a):
+    return jnp.swapaxes(a, -1, -2)
+
+
 def shards(cotangent, incoming, upd_u, upd_v, saved_x, saved_h, norm_gain, w_gate, w_up, w_down):
     vm = pltpu.VMEM
     dma = pltpu.SemaphoreType.DMA
@@ -389,20 +380,16 @@
         in_specs=[pl.BlockSpec(memory_space=pl.ANY)] * 10,
         out_specs=[pl.BlockSpec(memory_space=pltpu.VMEM)] * 2,
         scratch_shapes=[
-            vm((ROWS, CHUNK), f32),
-            vm((ROWS, CHUNK), f32),
-            vm((UPD, ROWS, CHUNK), f32),
-            vm((UPD, ROWS, CHUNK), f32),
-            vm((MB, ROWS, CHUNK), bf16),
+            vm(tile, f32),
+            vm(tile, f32),
+            vm((UPD, *tile), f32),
+            vm((UPD, *tile), f32),
+            vm((MB, *tile), bf16),
             vm((MB, 2, ROWS, HID), bf16),
             vm((1, CHUNK), f32),
             vm((2, FEATS, HALF), bf16),
             vm((2, FEATS, HALF), bf16),
             vm((ROW, PIECE, FEATS), bf16),
-            vm(tile, f32),
-            vm(tile, f32),
-            vm((UPD, *tile), f32),
-            vm((UPD, *tile), f32),
             vm((MB, *tile), f32),
             vm(tile, f32),
             vm((COL, MB, *tile), bf16),
@@ -449,7 +436,7 @@
         ),
         name="broyden",
     )(
-        cotangent, incoming, upd_u, upd_v, saved_x, saved_h, norm_gain,
+        turned(cotangent), turned(incoming), turned(upd_u), turned(upd_v), turned(saved_x), saved_h, norm_gain,
         w_gate, w_up, w_down.reshape(1, ROW, PIECE, FEATS),
     )
     return new.T[None], res.T[None]

time: 197 us -> 188 us (0.954)
  local copies, waits for them, and re-layouts: 11.2 us -> 2.75 us
    unnamed x7 -> x2, local copies, waits for them, and re-layouts: 11.2 us -> 2.75 us
where the time goes in v2:
time: 188 us
  Pallas kernels  184 us (98%)
  local copies, waits for them, and re-layouts  2.75 us (1%)
    pallas_call x1, Pallas kernels, shards(): pl.pallas_call(kernel, out_shape=[jax.ShapeDtypeStruct(tile, f32)] * 2, i...  184 us

profile of v2, /device:TPU:1, one launch (start us, length us, event | category | flops | bytes accessed | tf_op | source)
XLA Modules:
  0.0 187.7 jit_solution(5663878260795835809)
XLA Ops:
  0.6 184.3 %broyden.1 = (f32[64,128]{1,0:T(8,128)}, f32[64,128]{1,0:T(8,128)}) custom-call(f32[1,64,128]{2,1,0:T(8,128)} %bitcast.16, f32[1,64,128]{2,1,0:T(8,128)} %bitcast.17, f32[1,8,64,128]{3,2,1,0:T(8,128)} %bitcast.13, f32[1,8,64,128]{3,2,1,0:T(8,128)} %bitcast.14, bf16[1,4,64,128]{3,2,1,0:T(8,128)(2,1)} %bitcast.15, bf16[1,4,2,128,1792]{4,3,2,1,0:T(8,128)(2,1)} %h_h.1, ...), custom_call_target="tpu_custom_call" | custom-call | tf_op jit(solution)/shard_map/broyden/pallas_call | solution.py:377
  184.9 1.4 copy.14
  186.3 1.4 copy.15

commit v3 on v2

--- a/solution.py
+++ b/solution.py
@@ -19,7 +19,11 @@
 PIECE = HID // ROW
 FAR_Z = (4, 3, 5, 2, 6, 1, 7)
 FAR_X = (2, 1, 3)
-SLOTS = MB + 3
+ORDER = [
+    ("H", 3), ("V", 3), ("S", 3), ("H", 2), ("V", 2), ("q", 0), ("P", 3), ("g", 0), ("F", 3), ("S", 2),
+    ("H", 1), ("V", 1), ("r", 0), ("U", 3), ("P", 2), ("F", 2), ("S", 1), ("H", 0), ("V", 0), ("U", 2),
+    ("P", 1), ("F", 1), ("S", 0), ("U", 1), ("P", 0), ("F", 0), ("U", 0),
+]
 
 eps = 1e-05
 bf16 = jnp.bfloat16
@@ -33,7 +37,7 @@
     cot_t, inc_t, u_t, v_t, x_v, h_v, gain_v, wg_v, wu_v, wd_v,
     x_t, gain_t, gx, slope,
     start, gy, gys, carry, after, d1s, d1r, own, xsd, xrv, mine, ga, grads, acc, zs, zr,
-    ixs, ixr, izs, izr, sqs, sqz, sqm, sqx, rstd, home, dxs, dxr, dzs, dzr,
+    kzs, kzr, kps, kpr, above, above_all, lean, below, sqs, sqz, sqm, sqx, rstd, home, khome, vxs, vxr, vzs, vzr, dxs, dxr, dzs, dzr,
     load, first, ss, rs, one_s, one_r,
 ):
     s = lax.axis_index("section")
@@ -59,6 +63,14 @@
 
     def left(ref, send):
         remote(ref, ref, send, one_r.at[0], (s, mate, c)).wait_send()
+
+    barrier = pltpu.get_barrier_semaphore()
+    for k in FAR_Z:
+        pl.semaphore_signal(barrier, inc=1, device_id=(s, r, at_col(k)), device_id_type=MESH)
+    for k in (2, 1, 3):
+        pl.semaphore_signal(barrier, inc=1, device_id=(lax.rem(s + k, SECTIONS), r, c), device_id_type=MESH)
+    for k in range(1, ROW):
+        pl.semaphore_signal(barrier, inc=1, device_id=(s, lax.rem(r + k, ROW), c), device_id_type=MESH)
 
     loads = {}
     for i, (name, src, dst) in enumerate(
@@ -80,18 +92,9 @@
         loads[name] = pltpu.make_async_copy(src, dst, load.at[i])
         loads[name].start()
 
-    barrier = pltpu.get_barrier_semaphore()
-    for ds in range(SECTIONS):
-        for dc in range(COL):
-            if ds or dc:
-                there = (lax.rem(s + ds, SECTIONS), r, at_col(dc))
-                pl.semaphore_signal(barrier, inc=1, device_id=there, device_id_type=MESH)
-    for dr in range(1, ROW):
-        pl.semaphore_signal(barrier, inc=1, device_id=(s, lax.rem(r + dr, ROW), c), device_id_type=MESH)
-
     loads["cot"].wait()
     start[...] = cot_t[...].astype(bf16)
-    pl.semaphore_wait(barrier, SECTIONS * COL - 1 + ROW - 1)
+    pl.semaphore_wait(barrier, SECTIONS - 1 + COL - 1 + ROW - 1)
 
     LAST = SECTIONS - 1
     mb_home = s
@@ -101,16 +104,23 @@
         gy[LAST, c] = start[...]
         carry[LAST] = cot_t[...]
         for k in FAR_Z:
-            remote(start, gy.at[LAST, c], first.at[0], rs.at[0, LAST], (LAST, r, at_col(k))).start()
-
-    @pl.when(s != LAST)
-    def _():
-        for k in (*FAR_Z, 0):
-            remote(start, gy.at[mb_home, c], first.at[0], rs.at[0, mb_home], (LAST, r, at_col(k))).start()
-        remote(cot_t, carry.at[mb_home], first.at[1], rs.at[1, mb_home], (LAST, r, c)).start()
+            remote(
+                start, gy.at[LAST, c], first.at[0], rs.at[0, LAST], (LAST, r, at_col(k))
+            ).start()
+
+    loads["x"].wait()
+
+    @pl.when(s != 0)
+    def _():
+        remote(x_v, above, one_s.at[7], one_r.at[7], (s - 1, r, c)).start()
+
+    @pl.when(s == 0)
+    def _():
+        for m in range(1, MB):
+            remote(x_v.at[m], below, one_s.at[8], one_r.at[8], (m, r, c)).start()
+        below[...] = x_v[0]
 
     loads["gain"].wait()
-    loads["x"].wait()
     gain_t[...] = jnp.broadcast_to(gain_v[...], (ROWS, CHUNK)).T
     sums = []
     for m in range(MB):
@@ -122,8 +132,21 @@
     sqs[...] = sums
     sqz[c] = sums
     for k in FAR_Z:
+        remote(sqs, sqz.at[c], one_s.at[2], one_r.at[2], (s, r, at_col(k))).start()
+
+    @pl.when(s != LAST)
+    def _():
+        arrived(sqz.at[pl.ds(0, COL - 1)], one_r.at[2])
+        for k in (*FAR_Z, 0):
+            remote(start, gy.at[mb_home, c], first.at[0], rs.at[0, mb_home], (LAST, r, at_col(k))).start()
+        remote(cot_t, carry.at[mb_home], first.at[1], rs.at[1, mb_home], (LAST, r, c)).start()
+        arrived(above, one_r.at[7])
+        above_all[c] = above[...]
+        for k in FAR_Z:
+            remote(above, above_all.at[c], one_s.at[9], one_r.at[9], (s, r, at_col(k))).start()
+
+    for k in FAR_Z:
         remote(gx.at[c], gx.at[c], one_s.at[1], one_r.at[1], (s, r, at_col(k))).start()
-        remote(sqs, sqz.at[c], one_s.at[2], one_r.at[2], (s, r, at_col(k))).start()
 
     def slopes(m):
         for half in range(2):
@@ -155,22 +178,71 @@
     for name in ("wd", "wg0", "wg1", "wu0", "wu1"):
         loads[name].wait()
 
+    @pl.when(s != LAST)
+    def _():
+        arrived(above_all.at[pl.ds(0, COL - 1)], one_r.at[9])
+
+        def body(m, carry_):
+            a = above_all[:, m].reshape(FEATS, ROWS)
+            for i in range(ROW):
+                lean[m, i] = jnp.dot(wd_v[i], a, preferred_element_type=f32)
+            return carry_
+
+        lax.fori_loop(0, MB, body, 0)
+
+    def leanings():
+        @pl.when(s != 0)
+        def _():
+            arrived(below, one_r.at[8])
+
+        b = below[...].astype(f32)
+        part = jnp.concatenate([jnp.sum(v_t[i] * b, axis=0, keepdims=True) for i in range(UPD)], axis=0)
+        vxs[...] = part
+        vxr[r] = part
+        for k in range(1, ROW):
+            remote(vxs, vxr.at[r], one_s.at[11], one_r.at[11], (s, lax.rem(r + k, ROW), c)).start()
+        arrived(vxr.at[pl.ds(0, ROW - 1)], one_r.at[11])
+        part = jnp.sum(vxr[...], axis=0)
+        vzs[...] = part
+        vzr[c] = part
+        for k in FAR_Z:
+            remote(vzs, vzr.at[c], one_s.at[12], one_r.at[12], (s, r, at_col(k))).start()
+        arrived(vzr.at[pl.ds(0, COL - 1)], one_r.at[12])
+
+    @pl.when(s != LAST)
+    def _():
+        leanings()
+
     def hidden(m):
-        @pl.when(jnp.logical_and(s == LAST, m == LAST))
-        def _():
-            arrived(gy.at[m, pl.ds(0, COL - 1)], rs.at[0, m])
-
-        @pl.when(jnp.logical_not(jnp.logical_and(s == LAST, m == LAST)))
+        @pl.when(s == LAST)
+        def _():
+            if m == LAST:
+                arrived(gy.at[m, pl.ds(0, COL - 1)], rs.at[0, m])
+            else:
+                arrived(gy.at[m], rs.at[0, m])
+                arrived(carry.at[m], rs.at[1, m])
+            g = gy[m].reshape(FEATS, ROWS)
+            for i in range(XS):
+                d1s[m, i] = jnp.dot(wd_v[(1 - core) * XS + i], g, preferred_element_type=f32).astype(bf16)
+            remote(d1s.at[m], d1r.at[m], ss.at[2, m], rs.at[2, m], (s, mate, c)).start()
+            for i in range(XS):
+                own[m, i] = jnp.dot(wd_v[core * XS + i], g, preferred_element_type=f32)
+
+        @pl.when(s != LAST)
         def _():
             arrived(gy.at[m], rs.at[0, m])
+            arrived(kpr.at[m], rs.at[7, m])
             arrived(carry.at[m], rs.at[1, m])
-
-        g = gy[m].reshape(FEATS, ROWS)
-        for i in range(XS):
-            d1s[m, i] = jnp.dot(wd_v[(1 - core) * XS + i], g, preferred_element_type=f32).astype(bf16)
-        remote(d1s.at[m], d1r.at[m], ss.at[2, m], rs.at[2, m], (s, mate, c)).start()
-        for i in range(XS):
-            own[m, i] = jnp.dot(wd_v[core * XS + i], g, preferred_element_type=f32)
+            k = jnp.sum(kpr[m], axis=0)
+            g = gy[m].reshape(FEATS, ROWS)
+            for i in range(XS):
+                q = (1 - core) * XS + i
+                d1s[m, i] = (jnp.dot(wd_v[q], g, preferred_element_type=f32) - k * lean[m, q]).astype(bf16)
+            remote(d1s.at[m], d1r.at[m], ss.at[2, m], rs.at[2, m], (s, mate, c)).start()
+            for i in range(XS):
+                q = core * XS + i
+                own[m, i] = jnp.dot(wd_v[q], g, preferred_element_type=f32) - k * lean[m, q]
+            carry[m] = carry[m] - k * above[m].astype(f32)
 
     def halved(m):
         arrived(d1r.at[m], rs.at[2, m])
@@ -222,46 +294,48 @@
         for k in FAR_Z:
             to = at_col(k)
             remote(zs.at[m, to], zr.at[m, c], ss.at[6, m], rs.at[6, m], (s, r, to)).start()
+        kzs[m] = inner
+        for k in FAR_Z:
+            remote(kzs.at[m], kzr.at[m, c], ss.at[8, m], rs.at[8, m], (s, r, at_col(k))).start()
         zr[m, c] = zs[m, c]
-        ixs[m] = inner
-        ixr[m, r] = inner
-        for k in range(1, ROW):
-            remote(ixs.at[m], ixr.at[m, r], ss.at[7, m], rs.at[7, m], (s, lax.rem(r + k, ROW), c)).start()
-
-    def projected(m):
-        arrived(ixr.at[m, pl.ds(0, ROW - 1)], rs.at[7, m])
-        inner = jnp.sum(ixr[m], axis=0)
-        izs[m] = inner
-        izr[m, c] = inner
-        for k in FAR_Z:
-            remote(izs.at[m], izr.at[m, c], ss.at[8, m], rs.at[8, m], (s, r, at_col(k))).start()
+        kzr[m, c] = inner
 
     def updated(m):
         arrived(zr.at[m, pl.ds(0, COL - 1)], rs.at[6, m])
-        arrived(izr.at[m, pl.ds(0, COL - 1)], rs.at[8, m])
+        arrived(kzr.at[m, pl.ds(0, COL - 1)], rs.at[8, m])
         total = jnp.sum(zr[m].astype(f32), axis=0)
-        inner = jnp.sum(izr[m], axis=0) / D
+        inner = jnp.sum(kzr[m], axis=0)
         root = rstd[m]
-        fresh = carry[m] + root * (gain_t[...] * total) - x_t[m] * (root * root * root) * inner
+        fresh = carry[m] + root * (gain_t[...] * total)
         after[m] = fresh
+        kps[m] = (root * root * root) * (inner / D)
 
         @pl.when(s != 0)
         def _():
             gys[m] = fresh.astype(bf16)
             for k in (*FAR_Z, 0):
-                remote(gys.at[m], gy.at[m, c], ss.at[0, m], rs.at[0, m], (s - 1, r, at_col(k))).start()
+                remote(
+                    gys.at[m], gy.at[m, c], ss.at[0, m], rs.at[0, m], (s - 1, r, at_col(k))
+                ).start()
+            for k in range(ROW):
+                remote(kps.at[m], kpr.at[m, r], ss.at[7, m], rs.at[7, m], (s - 1, lax.rem(r + k, ROW), c)).start()
             remote(after.at[m], carry.at[m], ss.at[1, m], rs.at[1, m], (s - 1, r, c)).start()
 
-        @pl.when(jnp.logical_and(s == 0, m != 0))
-        def _():
-            remote(after.at[m], home, ss.at[1, m], one_r.at[4], (m, r, c)).start()
-
-        @pl.when(jnp.logical_and(s == 0, m == 0))
-        def _():
-            home[...] = fresh
+        @pl.when(s == 0)
+        def _():
+            if m == 0:
+                home[...] = fresh
+                khome[r] = kps[m]
+            else:
+                remote(after.at[m], home, ss.at[1, m], one_r.at[4], (m, r, c)).start()
+            for k in range(1 if m == 0 else 0, ROW):
+                remote(kps.at[m], khome.at[r], ss.at[7, m], one_r.at[10], (m, lax.rem(r + k, ROW), c)).start()
 
     def squares_met():
-        arrived(sqz.at[pl.ds(0, COL - 1)], one_r.at[2])
+        @pl.when(s == LAST)
+        def _():
+            arrived(sqz.at[pl.ds(0, COL - 1)], one_r.at[2])
+
         total = jnp.sum(sqz[...], axis=0)
         sqm[...] = total
         sqx[r] = total
@@ -270,49 +344,36 @@
 
     def roots():
         arrived(sqx.at[pl.ds(0, ROW - 1)], one_r.at[3])
-        arrived(gx.at[pl.ds(0, COL - 1)], one_r.at[1])
         root = lax.rsqrt(jnp.sum(sqx[...], axis=0) / D + eps)
         for m in range(MB):
             rstd[m] = root[m : m + 1]
 
-    def slot(t, carry_):
-        def stage(lag, body):
-            @pl.when(jnp.logical_and(t >= lag, t < lag + MB))
-            def _():
-                body(LAST - (t - lag))
-
-        stage(0, hidden)
-
-        @pl.when(t == 0)
-        def _():
+    stages = {"H": hidden, "V": halved, "S": summed, "P": spread, "F": features, "U": updated}
+    for step, m in ORDER:
+        if step == "q":
             squares_met()
-
-        stage(2, spread)
-        stage(1, summed)
-        stage(0, halved)
-
-        @pl.when(jnp.logical_and(s == LAST, t < LAST))
-        def _():
-            slopes(LAST - 1 - t)
-
-        @pl.when(t == 1)
-        def _():
+        elif step == "r":
             roots()
-
-        stage(2, features)
-        stage(3, updated)
-        stage(2, projected)
-        return carry_
-
-    lax.fori_loop(0, SLOTS, slot, 0)
+        elif step == "g":
+            arrived(gx.at[pl.ds(0, COL - 1)], one_r.at[1])
+        else:
+            stages[step](m)
+        if step == "V" and m:
+
+            @pl.when(s == LAST)
+            def _(m=m - 1):
+                slopes(m)
+
+    @pl.when(s == LAST)
+    def _():
+        leanings()
 
     @pl.when(s != 0)
     def _():
         arrived(home, one_r.at[4])
 
-    resid = home[...] + inc_t[...] - cot_t[...]
-    res_o[...] = resid
-    part = jnp.concatenate([jnp.sum(v_t[i] * resid, axis=0, keepdims=True) for i in range(UPD)], axis=0)
+    rough = home[...] + inc_t[...] - cot_t[...]
+    part = jnp.concatenate([jnp.sum(v_t[i] * rough, axis=0, keepdims=True) for i in range(UPD)], axis=0)
     dxs[...] = part
     dxr[r] = part
     for k in range(1, ROW):
@@ -323,8 +384,21 @@
     dzr[c] = part
     for k in FAR_Z:
         remote(dzs, dzr.at[c], one_s.at[6], one_r.at[6], (s, r, at_col(k))).start()
+
+    @pl.when(s != 0)
+    def _():
+        arrived(khome, one_r.at[10])
+
+    @pl.when(s == 0)
+    def _():
+        arrived(khome.at[pl.ds(0, ROW - 1)], one_r.at[10])
+
+    k_all = jnp.sum(khome[...], axis=0)
+    resid = home[...] - k_all * below[...].astype(f32) + inc_t[...] - cot_t[...]
+    res_o[...] = resid
+    tilt = k_all * jnp.sum(vzr[...], axis=0)
     arrived(dzr.at[pl.ds(0, COL - 1)], one_r.at[6])
-    dots = jnp.sum(jnp.sum(dzr[...], axis=0), axis=1, keepdims=True)
+    dots = jnp.sum(jnp.sum(dzr[...], axis=0) - tilt, axis=1, keepdims=True)
     update = dots[0:1] * u_t[0]
     for i in range(1, UPD):
         update = update + dots[i : i + 1] * u_t[i]
@@ -338,10 +412,21 @@
     def _():
         left(gy.at[0], first.at[0])
         left(cot_t, first.at[1])
+        left(above_all.at[pl.ds(0, COL - 1)], one_s.at[9])
+
+    @pl.when(s != 0)
+    def _():
+        left(x_v, one_s.at[7])
+
+    @pl.when(s == 0)
+    def _():
+        left(x_v.at[pl.ds(1, MB - 1)], one_s.at[8])
 
     left(gx.at[pl.ds(0, COL - 1)], one_s.at[1])
     left(sqz.at[pl.ds(0, COL - 1)], one_s.at[2])
     left(sqx.at[pl.ds(0, ROW - 1)], one_s.at[3])
+    left(vxr.at[pl.ds(0, ROW - 1)], one_s.at[11])
+    left(vzr.at[pl.ds(0, COL - 1)], one_s.at[12])
     left(dxr.at[pl.ds(0, ROW - 1)], one_s.at[5])
     left(dzr.at[pl.ds(0, COL - 1)], one_s.at[6])
 
@@ -353,14 +438,18 @@
         @pl.when(jnp.logical_or(s != 0, m != 0))
         def _():
             left(after.at[m], ss.at[1, m])
+            left(kpr.at[m], ss.at[7, m])
+
+        @pl.when(jnp.logical_and(s == 0, m == 0))
+        def _():
+            left(kpr.at[m, pl.ds(0, ROW - 1)], ss.at[7, m])
 
         left(d1s.at[m], ss.at[2, m])
         left(xrv.at[m, pl.ds(0, XS - 1)], ss.at[3, m])
         left(ga.at[m, core, pl.ds(0, XS - 1)], ss.at[4, m])
         left(ga.at[m, core], ss.at[5, m])
         left(zr.at[m, pl.ds(0, COL - 1)], ss.at[6, m])
-        left(ixr.at[m, pl.ds(0, ROW - 1)], ss.at[7, m])
-        left(izr.at[m, pl.ds(0, COL - 1)], ss.at[8, m])
+        left(kzr.at[m, pl.ds(0, COL - 1)], ss.at[8, m])
         return carry_
 
     lax.fori_loop(0, MB, drained, 0)
@@ -411,15 +500,24 @@
             vm((MB, COL, *tile), bf16),
             vm((MB, COL, *tile), bf16),
             vm((MB, 1, ROWS), f32),
+            vm((MB, COL, 1, ROWS), f32),
+            vm((MB, 1, ROWS), f32),
             vm((MB, ROW, 1, ROWS), f32),
-            vm((MB, 1, ROWS), f32),
-            vm((MB, COL, 1, ROWS), f32),
+            vm((MB, *tile), bf16),
+            vm((COL, MB, *tile), bf16),
+            vm((MB, ROW, PIECE, ROWS), f32),
+            vm(tile, bf16),
             vm((8, ROWS), f32),
             vm((COL, 8, ROWS), f32),
             vm((8, ROWS), f32),
             vm((ROW, 8, ROWS), f32),
             vm((MB, 1, ROWS), f32),
             vm(tile, f32),
+            vm((ROW, 1, ROWS), f32),
+            vm((UPD, ROWS), f32),
+            vm((ROW, UPD, ROWS), f32),
+            vm((UPD, ROWS), f32),
+            vm((COL, UPD, ROWS), f32),
             vm((UPD, ROWS), f32),
             vm((ROW, UPD, ROWS), f32),
             vm((UPD, ROWS), f32),
@@ -428,8 +526,8 @@
             dma((2,)),
             dma((9, MB)),
             dma((9, MB)),
-            dma((7,)),
-            dma((7,)),
+            dma((13,)),
+            dma((13,)),
         ],
         compiler_params=pltpu.CompilerParams(
             collective_id=0, has_side_effects=True, vmem_limit_bytes=60 * 1024 * 1024

time: 188 us -> 157 us (0.84)
  Pallas kernels: 184 us -> 153 us
    pallas_call x1, Pallas kernels: 184 us -> 153 us  [shards(): pl.pallas_call(kernel, out_shape=[jax.ShapeDtypeStruct(tile, f32)] * 2, i...]
where the time goes in v3:
time: 157 us
  Pallas kernels  153 us (97%)
  local copies, waits for them, and re-layouts  2.75 us (2%)
    pallas_call x1, Pallas kernels, shards(): pl.pallas_call(kernel, out_shape=[jax.ShapeDtypeStruct(tile, f32)] * 2, i...  153 us

profile of v3, /device:TPU:1, one launch (start us, length us, event | category | flops | bytes accessed | tf_op | source)
XLA Modules:
  0.0 156.8 jit_solution(3744356281644823373)
XLA Ops:
  0.6 153.4 %broyden.1 = (f32[64,128]{1,0:T(8,128)}, f32[64,128]{1,0:T(8,128)}) custom-call(f32[1,64,128]{2,1,0:T(8,128)} %bitcast.16, f32[1,64,128]{2,1,0:T(8,128)} %bitcast.17, f32[1,8,64,128]{3,2,1,0:T(8,128)} %bitcast.13, f32[1,8,64,128]{3,2,1,0:T(8,128)} %bitcast.14, bf16[1,4,64,128]{3,2,1,0:T(8,128)(2,1)} %bitcast.15, bf16[1,4,2,128,1792]{4,3,2,1,0:T(8,128)(2,1)} %h_h.1, ...), custom_call_target="tpu_custom_call" | custom-call | tf_op jit(solution)/shard_map/broyden/pallas_call | solution.py:466
  154.0 1.4 copy.14
  155.4 1.4 copy.15

commit v4 on v3

--- a/solution.py
+++ b/solution.py
@@ -19,11 +19,16 @@
 PIECE = HID // ROW
 FAR_Z = (4, 3, 5, 2, 6, 1, 7)
 FAR_X = (2, 1, 3)
-ORDER = [
+FIRST_ORDER = [
     ("H", 3), ("V", 3), ("S", 3), ("H", 2), ("V", 2), ("q", 0), ("P", 3), ("g", 0), ("F", 3), ("S", 2),
     ("H", 1), ("V", 1), ("r", 0), ("U", 3), ("P", 2), ("F", 2), ("S", 1), ("H", 0), ("V", 0), ("U", 2),
     ("P", 1), ("F", 1), ("S", 0), ("U", 1), ("P", 0), ("F", 0), ("U", 0),
 ]
+ORDER = [
+    ("H", 3), ("V", 3), ("S", 3), ("H", 2), ("V", 2), ("q", 0), ("P", 3), ("g", 0), ("F", 3), ("S", 2),
+    ("H", 1), ("V", 1), ("r", 0), ("U", 3), ("P", 2), ("F", 2), ("S", 1), ("H", 0), ("V", 0), ("U", 2),
+    ("P", 1), ("F", 1), ("S", 0), ("U", 1), ("P", 0), ("F", 0), ("e", 0), ("d", 0), ("U", 0),
+]
 
 eps = 1e-05
 bf16 = jnp.bfloat16
@@ -35,9 +40,9 @@
     cot_h, inc_h, u_h, v_h, x_h, h_h, gain_h, wg_h, wu_h, wd_h,
     new_o, res_o,
     cot_t, inc_t, u_t, v_t, x_v, h_v, gain_v, wg_v, wu_v, wd_v,
-    x_t, gain_t, gx, slope,
+    x_t, gain_t, gx, gv, slope,
     start, gy, gys, carry, after, d1s, d1r, own, xsd, xrv, mine, ga, grads, acc, zs, zr,
-    kzs, kzr, kps, kpr, above, above_all, lean, below, sqs, sqz, sqm, sqx, rstd, home, khome, vxs, vxr, vzs, vzr, dxs, dxr, dzs, dzr,
+    kzs, kzr, kps, kpr, above, above_all, lean, below, sqs, sqz, sqm, sqx, rstd, home, khome, kall, vxs, vxr, vzs, vzr, dxs, dxr, dzs, dzr,
     load, first, ss, rs, one_s, one_r,
 ):
     s = lax.axis_index("section")
@@ -178,18 +183,6 @@
     for name in ("wd", "wg0", "wg1", "wu0", "wu1"):
         loads[name].wait()
 
-    @pl.when(s != LAST)
-    def _():
-        arrived(above_all.at[pl.ds(0, COL - 1)], one_r.at[9])
-
-        def body(m, carry_):
-            a = above_all[:, m].reshape(FEATS, ROWS)
-            for i in range(ROW):
-                lean[m, i] = jnp.dot(wd_v[i], a, preferred_element_type=f32)
-            return carry_
-
-        lax.fori_loop(0, MB, body, 0)
-
     def leanings():
         @pl.when(s != 0)
         def _():
@@ -213,35 +206,50 @@
     def _():
         leanings()
 
-    def hidden(m):
-        @pl.when(s == LAST)
-        def _():
-            if m == LAST:
-                arrived(gy.at[m, pl.ds(0, COL - 1)], rs.at[0, m])
-            else:
-                arrived(gy.at[m], rs.at[0, m])
-                arrived(carry.at[m], rs.at[1, m])
-            g = gy[m].reshape(FEATS, ROWS)
-            for i in range(XS):
-                d1s[m, i] = jnp.dot(wd_v[(1 - core) * XS + i], g, preferred_element_type=f32).astype(bf16)
-            remote(d1s.at[m], d1r.at[m], ss.at[2, m], rs.at[2, m], (s, mate, c)).start()
-            for i in range(XS):
-                own[m, i] = jnp.dot(wd_v[core * XS + i], g, preferred_element_type=f32)
-
-        @pl.when(s != LAST)
-        def _():
+    @pl.when(s == 0)
+    def _():
+        for i in range(UPD):
+            gv[c, i] = (gain_t[...] * v_t[i]).astype(bf16)
+        for k in FAR_Z:
+            remote(gv.at[c], gv.at[c], one_s.at[13], one_r.at[13], (s, r, at_col(k))).start()
+
+    @pl.when(s != LAST)
+    def _():
+        arrived(above_all.at[pl.ds(0, COL - 1)], one_r.at[9])
+
+        def body(m, carry_):
+            a = above_all[:, m].reshape(FEATS, ROWS)
+            for i in range(ROW):
+                lean[m, i] = jnp.dot(wd_v[i], a, preferred_element_type=f32)
+            return carry_
+
+        lax.fori_loop(0, MB, body, 0)
+
+    @pl.when(s == 0)
+    def _():
+        arrived(gv.at[pl.ds(0, COL - 1)], one_r.at[13])
+
+    def hidden(m, first):
+        if first and m == LAST:
+            arrived(gy.at[m, pl.ds(0, COL - 1)], rs.at[0, m])
+        else:
             arrived(gy.at[m], rs.at[0, m])
+            arrived(carry.at[m], rs.at[1, m])
+        if not first:
             arrived(kpr.at[m], rs.at[7, m])
-            arrived(carry.at[m], rs.at[1, m])
             k = jnp.sum(kpr[m], axis=0)
-            g = gy[m].reshape(FEATS, ROWS)
-            for i in range(XS):
-                q = (1 - core) * XS + i
-                d1s[m, i] = (jnp.dot(wd_v[q], g, preferred_element_type=f32) - k * lean[m, q]).astype(bf16)
-            remote(d1s.at[m], d1r.at[m], ss.at[2, m], rs.at[2, m], (s, mate, c)).start()
-            for i in range(XS):
-                q = core * XS + i
-                own[m, i] = jnp.dot(wd_v[q], g, preferred_element_type=f32) - k * lean[m, q]
+        g = gy[m].reshape(FEATS, ROWS)
+
+        def product(q):
+            whole = jnp.dot(wd_v[q], g, preferred_element_type=f32)
+            return whole if first else whole - k * lean[m, q]
+
+        for i in range(XS):
+            d1s[m, i] = product((1 - core) * XS + i).astype(bf16)
+        remote(d1s.at[m], d1r.at[m], ss.at[2, m], rs.at[2, m], (s, mate, c)).start()
+        for i in range(XS):
+            own[m, i] = product(core * XS + i)
+        if not first:
             carry[m] = carry[m] - k * above[m].astype(f32)
 
     def halved(m):
@@ -291,6 +299,8 @@
             scaled = gx[pl.ds(4 * b, 4), m].reshape(256, ROWS).astype(f32)
             inner = inner + jnp.sum(part * scaled, axis=0, keepdims=True)
             zs[m, pl.ds(4 * b, 4)] = part.astype(bf16).reshape(4, CHUNK, ROWS)
+            if m == 0:
+                acc[rows] = part
         for k in FAR_Z:
             to = at_col(k)
             remote(zs.at[m, to], zr.at[m, c], ss.at[6, m], rs.at[6, m], (s, r, to)).start()
@@ -299,6 +309,31 @@
             remote(kzs.at[m], kzr.at[m, c], ss.at[8, m], rs.at[8, m], (s, r, at_col(k))).start()
         zr[m, c] = zs[m, c]
         kzr[m, c] = inner
+
+    def early():
+        known = carry[0] + inc_t[...] - cot_t[...]
+        found = []
+        for i in range(UPD):
+            total = jnp.zeros((1, ROWS), f32)
+            for b in range(2):
+                scaled = gv[pl.ds(4 * b, 4), i].reshape(256, ROWS).astype(f32)
+                total = total + jnp.sum(acc[pl.ds(b * 256, 256)] * scaled, axis=0, keepdims=True)
+            found.append(rstd[0] * total + jnp.sum(v_t[i] * known, axis=0, keepdims=True))
+        meet_row(jnp.concatenate([*found, kzs[0], jnp.zeros((7, ROWS), f32)], axis=0))
+
+    def meet_row(part):
+        dxs[...] = part
+        dxr[r] = part
+        for k in range(1, ROW):
+            remote(dxs, dxr.at[r], one_s.at[5], one_r.at[5], (s, lax.rem(r + k, ROW), c)).start()
+
+    def meet_col():
+        arrived(dxr.at[pl.ds(0, ROW - 1)], one_r.at[5])
+        part = jnp.sum(dxr[...], axis=0)
+        dzs[...] = part
+        dzr[c] = part
+        for k in FAR_Z:
+            remote(dzs, dzr.at[c], one_s.at[6], one_r.at[6], (s, r, at_col(k))).start()
 
     def updated(m):
         arrived(zr.at[m, pl.ds(0, COL - 1)], rs.at[6, m])
@@ -325,17 +360,12 @@
         def _():
             if m == 0:
                 home[...] = fresh
-                khome[r] = kps[m]
             else:
                 remote(after.at[m], home, ss.at[1, m], one_r.at[4], (m, r, c)).start()
-            for k in range(1 if m == 0 else 0, ROW):
-                remote(kps.at[m], khome.at[r], ss.at[7, m], one_r.at[10], (m, lax.rem(r + k, ROW), c)).start()
+                for k in range(ROW):
+                    remote(kps.at[m], khome.at[r], ss.at[7, m], one_r.at[10], (m, lax.rem(r + k, ROW), c)).start()
 
     def squares_met():
-        @pl.when(s == LAST)
-        def _():
-            arrived(sqz.at[pl.ds(0, COL - 1)], one_r.at[2])
-
         total = jnp.sum(sqz[...], axis=0)
         sqm[...] = total
         sqx[r] = total
@@ -348,57 +378,69 @@
         for m in range(MB):
             rstd[m] = root[m : m + 1]
 
-    stages = {"H": hidden, "V": halved, "S": summed, "P": spread, "F": features, "U": updated}
-    for step, m in ORDER:
-        if step == "q":
-            squares_met()
-        elif step == "r":
-            roots()
-        elif step == "g":
-            arrived(gx.at[pl.ds(0, COL - 1)], one_r.at[1])
-        else:
-            stages[step](m)
-        if step == "V" and m:
-
-            @pl.when(s == LAST)
-            def _(m=m - 1):
-                slopes(m)
+    stages = {"V": halved, "S": summed, "P": spread, "F": features, "U": updated}
+
+    def play(order, first):
+        for step, m in order:
+            if step == "H":
+                hidden(m, first)
+            elif step == "q":
+                if first:
+                    arrived(sqz.at[pl.ds(0, COL - 1)], one_r.at[2])
+                squares_met()
+            elif step == "r":
+                roots()
+            elif step == "g":
+                arrived(gx.at[pl.ds(0, COL - 1)], one_r.at[1])
+            elif step == "e":
+
+                @pl.when(s == 0)
+                def _():
+                    early()
+
+            elif step == "d":
+
+                @pl.when(s == 0)
+                def _():
+                    meet_col()
+
+            else:
+                stages[step](m)
+            if step == "V" and m and first:
+                slopes(m - 1)
 
     @pl.when(s == LAST)
     def _():
+        play(FIRST_ORDER, True)
+
+    @pl.when(s != LAST)
+    def _():
+        play(ORDER, False)
+
+    @pl.when(s == LAST)
+    def _():
         leanings()
 
     @pl.when(s != 0)
     def _():
         arrived(home, one_r.at[4])
-
-    rough = home[...] + inc_t[...] - cot_t[...]
-    part = jnp.concatenate([jnp.sum(v_t[i] * rough, axis=0, keepdims=True) for i in range(UPD)], axis=0)
-    dxs[...] = part
-    dxr[r] = part
-    for k in range(1, ROW):
-        remote(dxs, dxr.at[r], one_s.at[5], one_r.at[5], (s, lax.rem(r + k, ROW), c)).start()
-    arrived(dxr.at[pl.ds(0, ROW - 1)], one_r.at[5])
-    part = jnp.sum(dxr[...], axis=0)
-    dzs[...] = part
-    dzr[c] = part
-    for k in FAR_Z:
-        remote(dzs, dzr.at[c], one_s.at[6], one_r.at[6], (s, r, at_col(k))).start()
-
-    @pl.when(s != 0)
-    def _():
+        rough = home[...] + inc_t[...] - cot_t[...]
+        part = [jnp.sum(v_t[i] * rough, axis=0, keepdims=True) for i in range(UPD)]
+        meet_row(jnp.concatenate([*part, jnp.zeros((8, ROWS), f32)], axis=0))
+        meet_col()
         arrived(khome, one_r.at[10])
+        kall[...] = jnp.sum(khome[...], axis=0)
+
+    arrived(dzr.at[pl.ds(0, COL - 1)], one_r.at[6])
+    met = jnp.sum(dzr[...], axis=0)
 
     @pl.when(s == 0)
     def _():
-        arrived(khome.at[pl.ds(0, ROW - 1)], one_r.at[10])
-
-    k_all = jnp.sum(khome[...], axis=0)
-    resid = home[...] - k_all * below[...].astype(f32) + inc_t[...] - cot_t[...]
+        kall[...] = (rstd[0] * rstd[0] * rstd[0]) * (met[UPD : UPD + 1] / D)
+
+    resid = home[...] - kall[...] * below[...].astype(f32) + inc_t[...] - cot_t[...]
     res_o[...] = resid
-    tilt = k_all * jnp.sum(vzr[...], axis=0)
-    arrived(dzr.at[pl.ds(0, COL - 1)], one_r.at[6])
-    dots = jnp.sum(jnp.sum(dzr[...], axis=0) - tilt, axis=1, keepdims=True)
+    dots = jnp.sum(met[:UPD] - kall[...] * jnp.sum(vzr[...], axis=0), axis=1, keepdims=True)
     update = dots[0:1] * u_t[0]
     for i in range(1, UPD):
         update = update + dots[i : i + 1] * u_t[i]
@@ -420,6 +462,7 @@
 
     @pl.when(s == 0)
     def _():
+        left(gv.at[pl.ds(0, COL - 1)], one_s.at[13])
         left(x_v.at[pl.ds(1, MB - 1)], one_s.at[8])
 
     left(gx.at[pl.ds(0, COL - 1)], one_s.at[1])
@@ -439,10 +482,6 @@
         def _():
             left(after.at[m], ss.at[1, m])
             left(kpr.at[m], ss.at[7, m])
-
-        @pl.when(jnp.logical_and(s == 0, m == 0))
-        def _():
-            left(kpr.at[m, pl.ds(0, ROW - 1)], ss.at[7, m])
 
         left(d1s.at[m], ss.at[2, m])
         left(xrv.at[m, pl.ds(0, XS - 1)], ss.at[3, m])
@@ -482,6 +521,7 @@
             vm((MB, *tile), f32),
             vm(tile, f32),
             vm((COL, MB, *tile), bf16),
+            vm((COL, UPD, *tile), bf16),
             vm((MB, 2, 2, HALF, ROWS), f32),
             vm(tile, bf16),
             vm((MB, COL, *tile), bf16),
@@ -514,20 +554,21 @@
             vm((MB, 1, ROWS), f32),
             vm(tile, f32),
             vm((ROW, 1, ROWS), f32),
+            vm((1, ROWS), f32),
             vm((UPD, ROWS), f32),
             vm((ROW, UPD, ROWS), f32),
             vm((UPD, ROWS), f32),
             vm((COL, UPD, ROWS), f32),
-            vm((UPD, ROWS), f32),
-            vm((ROW, UPD, ROWS), f32),
-            vm((UPD, ROWS), f32),
-            vm((COL, UPD, ROWS), f32),
+            vm((2 * UPD, ROWS), f32),
+            vm((ROW, 2 * UPD, ROWS), f32),
+            vm((2 * UPD, ROWS), f32),
+            vm((COL, 2 * UPD, ROWS), f32),
             dma((12,)),
             dma((2,)),
             dma((9, MB)),
             dma((9, MB)),
-            dma((13,)),
-            dma((13,)),
+            dma((14,)),
+            dma((14,)),
         ],
         compiler_params=pltpu.CompilerParams(
             collective_id=0, has_side_effects=True, vmem_limit_bytes=60 * 1024 * 1024

time: 157 us -> 152 us (0.968)
  Pallas kernels: 153 us -> 149 us
    pallas_call x1, Pallas kernels: 153 us -> 149 us  [shards(): pl.pallas_call(kernel, out_shape=[jax.ShapeDtypeStruct(tile, f32)] * 2, i...]
where the time goes in v4:
time: 152 us
  Pallas kernels  149 us (98%)
  local copies, waits for them, and re-layouts  2.75 us (2%)
    pallas_call x1, Pallas kernels, shards(): pl.pallas_call(kernel, out_shape=[jax.ShapeDtypeStruct(tile, f32)] * 2, i...  149 us

profile of v4, /device:TPU:1, one launch (start us, length us, event | category | flops | bytes accessed | tf_op | source)
XLA Modules:
  0.0 152.1 jit_solution(13862576502873245802)
XLA Ops:
  0.6 148.7 %broyden.1 = (f32[64,128]{1,0:T(8,128)}, f32[64,128]{1,0:T(8,128)}) custom-call(f32[1,64,128]{2,1,0:T(8,128)} %bitcast.16, f32[1,64,128]{2,1,0:T(8,128)} %bitcast.17, f32[1,8,64,128]{3,2,1,0:T(8,128)} %bitcast.13, f32[1,8,64,128]{3,2,1,0:T(8,128)} %bitcast.14, bf16[1,4,64,128]{3,2,1,0:T(8,128)(2,1)} %bitcast.15, bf16[1,4,2,128,1792]{4,3,2,1,0:T(8,128)(2,1)} %h_h.1, ...), custom_call_target="tpu_custom_call" | custom-call | tf_op jit(solution)/shard_map/broyden/pallas_call | solution.py:505
  149.3 1.4 copy.14
  150.7 1.4 copy.15

commit v5 on v4

--- a/solution.py
+++ b/solution.py
@@ -17,6 +17,8 @@
 HID = FF // COL
 HALF = HID // 2
 PIECE = HID // ROW
+PARTS = 2
+PART = PIECE // PARTS
 FAR_Z = (4, 3, 5, 2, 6, 1, 7)
 FAR_X = (2, 1, 3)
 FIRST_ORDER = [
@@ -38,12 +40,12 @@
 
 def kernel(
     cot_h, inc_h, u_h, v_h, x_h, h_h, gain_h, wg_h, wu_h, wd_h,
-    new_o, res_o,
+    out_o,
     cot_t, inc_t, u_t, v_t, x_v, h_v, gain_v, wg_v, wu_v, wd_v,
     x_t, gain_t, gx, gv, slope,
     start, gy, gys, carry, after, d1s, d1r, own, xsd, xrv, mine, ga, grads, acc, zs, zr,
     kzs, kzr, kps, kpr, above, above_all, lean, below, sqs, sqz, sqm, sqx, rstd, home, khome, kall, vxs, vxr, vzs, vzr, dxs, dxr, dzs, dzr,
-    load, first, ss, rs, one_s, one_r,
+    load, first, ss, rs, split, one_s, one_r,
 ):
     s = lax.axis_index("section")
     r = lax.axis_index("row")
@@ -194,13 +196,14 @@
         vxr[r] = part
         for k in range(1, ROW):
             remote(vxs, vxr.at[r], one_s.at[11], one_r.at[11], (s, lax.rem(r + k, ROW), c)).start()
+
+    def leanings_met():
         arrived(vxr.at[pl.ds(0, ROW - 1)], one_r.at[11])
         part = jnp.sum(vxr[...], axis=0)
         vzs[...] = part
         vzr[c] = part
         for k in FAR_Z:
             remote(vzs, vzr.at[c], one_s.at[12], one_r.at[12], (s, r, at_col(k))).start()
-        arrived(vzr.at[pl.ds(0, COL - 1)], one_r.at[12])
 
     @pl.when(s != LAST)
     def _():
@@ -224,6 +227,7 @@
             return carry_
 
         lax.fori_loop(0, MB, body, 0)
+        leanings_met()
 
     @pl.when(s == 0)
     def _():
@@ -240,34 +244,43 @@
             k = jnp.sum(kpr[m], axis=0)
         g = gy[m].reshape(FEATS, ROWS)
 
-        def product(q):
-            whole = jnp.dot(wd_v[q], g, preferred_element_type=f32)
-            return whole if first else whole - k * lean[m, q]
-
-        for i in range(XS):
-            d1s[m, i] = product((1 - core) * XS + i).astype(bf16)
-        remote(d1s.at[m], d1r.at[m], ss.at[2, m], rs.at[2, m], (s, mate, c)).start()
-        for i in range(XS):
-            own[m, i] = product(core * XS + i)
+        def product(q, b):
+            rows = pl.ds(b * PART, PART)
+            whole = jnp.dot(wd_v[q, rows], g, preferred_element_type=f32)
+            return whole if first else whole - k * lean[m, q, rows]
+
+        for b in range(PARTS):
+            for i in range(XS):
+                d1s[m, b, i] = product((1 - core) * XS + i, b).astype(bf16)
+            remote(d1s.at[m, b], d1r.at[m, b], ss.at[2, m], split.at[0, b, m], (s, mate, c)).start()
+        for b in range(PARTS):
+            for i in range(XS):
+                own[m, b, i] = product(core * XS + i, b)
         if not first:
             carry[m] = carry[m] - k * above[m].astype(f32)
 
     def halved(m):
-        arrived(d1r.at[m], rs.at[2, m])
-        for k in FAR_X:
-            to = at_x(k)
-            xsd[m, to] = (own[m, to] + d1r[m, to].astype(f32)).astype(bf16)
-            remote(xsd.at[m, to], xrv.at[m, x], ss.at[3, m], rs.at[3, m], (s, 2 * to + core, c)).start()
-        mine[m] = own[m, x] + d1r[m, x].astype(f32)
+        for b in range(PARTS):
+            arrived(d1r.at[m, b], split.at[0, b, m])
+            for k in FAR_X:
+                to = at_x(k)
+                xsd[m, b, to] = (own[m, b, to] + d1r[m, b, to].astype(f32)).astype(bf16)
+                remote(
+                    xsd.at[m, b, to], xrv.at[m, b, x], ss.at[3, m], split.at[1, b, m], (s, 2 * to + core, c)
+                ).start()
+            mine[m, b] = own[m, b, x] + d1r[m, b, x].astype(f32)
 
     def summed(m):
-        arrived(xrv.at[m, pl.ds(0, XS - 1)], rs.at[3, m])
-        total = mine[m]
-        for k in FAR_X:
-            total = total + xrv[m, at_x(k)].astype(f32)
-        ga[m, core, x] = total.astype(bf16)
-        for k in FAR_X:
-            remote(ga.at[m, core, x], ga.at[m, core, x], ss.at[4, m], rs.at[4, m], (s, 2 * at_x(k) + core, c)).start()
+        for b in range(PARTS):
+            arrived(xrv.at[m, b, pl.ds(0, XS - 1)], split.at[1, b, m])
+            total = mine[m, b]
+            for k in FAR_X:
+                total = total + xrv[m, b, at_x(k)].astype(f32)
+            ga[m, core, x, b] = total.astype(bf16)
+            for k in FAR_X:
+                remote(
+                    ga.at[m, core, x, b], ga.at[m, core, x, b], ss.at[4, m], rs.at[4, m], (s, 2 * at_x(k) + core, c)
+                ).start()
 
     def gradients(m, half):
         g = ga[m, half].reshape(HALF, ROWS).astype(f32)
@@ -420,6 +433,7 @@
     @pl.when(s == LAST)
     def _():
         leanings()
+        leanings_met()
 
     @pl.when(s != 0)
     def _():
@@ -431,6 +445,7 @@
         arrived(khome, one_r.at[10])
         kall[...] = jnp.sum(khome[...], axis=0)
 
+    arrived(vzr.at[pl.ds(0, COL - 1)], one_r.at[12])
     arrived(dzr.at[pl.ds(0, COL - 1)], one_r.at[6])
     met = jnp.sum(dzr[...], axis=0)
 
@@ -439,12 +454,12 @@
         kall[...] = (rstd[0] * rstd[0] * rstd[0]) * (met[UPD : UPD + 1] / D)
 
     resid = home[...] - kall[...] * below[...].astype(f32) + inc_t[...] - cot_t[...]
-    res_o[...] = resid
+    out_o[1] = resid
     dots = jnp.sum(met[:UPD] - kall[...] * jnp.sum(vzr[...], axis=0), axis=1, keepdims=True)
     update = dots[0:1] * u_t[0]
     for i in range(1, UPD):
         update = update + dots[i : i + 1] * u_t[i]
-    new_o[...] = cot_t[...] + resid - update
+    out_o[0] = cot_t[...] + resid - update
 
     @pl.when(s == LAST)
     def _():
@@ -484,7 +499,7 @@
             left(kpr.at[m], ss.at[7, m])
 
         left(d1s.at[m], ss.at[2, m])
-        left(xrv.at[m, pl.ds(0, XS - 1)], ss.at[3, m])
+        left(xrv.at[m, :, pl.ds(0, XS - 1)], ss.at[3, m])
         left(ga.at[m, core, pl.ds(0, XS - 1)], ss.at[4, m])
         left(ga.at[m, core], ss.at[5, m])
         left(zr.at[m, pl.ds(0, COL - 1)], ss.at[6, m])
@@ -502,11 +517,11 @@
     vm = pltpu.VMEM
     dma = pltpu.SemaphoreType.DMA
     tile = (CHUNK, ROWS)
-    new, res = pl.pallas_call(
+    out = pl.pallas_call(
         kernel,
-        out_shape=[jax.ShapeDtypeStruct(tile, f32)] * 2,
+        out_shape=jax.ShapeDtypeStruct((2, *tile), f32),
         in_specs=[pl.BlockSpec(memory_space=pl.ANY)] * 10,
-        out_specs=[pl.BlockSpec(memory_space=pltpu.VMEM)] * 2,
+        out_specs=pl.BlockSpec(memory_space=pltpu.VMEM),
         scratch_shapes=[
             vm(tile, f32),
             vm(tile, f32),
@@ -528,13 +543,13 @@
             vm((MB, *tile), bf16),
             vm((MB, *tile), f32),
             vm((MB, *tile), f32),
-            vm((MB, XS, PIECE, ROWS), bf16),
-            vm((MB, XS, PIECE, ROWS), bf16),
-            vm((MB, XS, PIECE, ROWS), f32),
-            vm((MB, XS, PIECE, ROWS), bf16),
-            vm((MB, XS, PIECE, ROWS), bf16),
-            vm((MB, PIECE, ROWS), f32),
-            vm((MB, 2, XS, PIECE, ROWS), bf16),
+            vm((MB, PARTS, XS, PART, ROWS), bf16),
+            vm((MB, PARTS, XS, PART, ROWS), bf16),
+            vm((MB, PARTS, XS, PART, ROWS), f32),
+            vm((MB, PARTS, XS, PART, ROWS), bf16),
+            vm((MB, PARTS, XS, PART, ROWS), bf16),
+            vm((MB, PARTS, PART, ROWS), f32),
+            vm((MB, 2, XS, PARTS, PART, ROWS), bf16),
             vm((2, HALF, ROWS), bf16),
             vm((FEATS, ROWS), f32),
             vm((MB, COL, *tile), bf16),
@@ -567,6 +582,7 @@
             dma((2,)),
             dma((9, MB)),
             dma((9, MB)),
+            dma((2, PARTS, MB)),
             dma((14,)),
             dma((14,)),
         ],
@@ -578,7 +594,7 @@
         turned(cotangent), turned(incoming), turned(upd_u), turned(upd_v), turned(saved_x), saved_h, norm_gain,
         w_gate, w_up, w_down.reshape(1, ROW, PIECE, FEATS),
     )
-    return new.T[None], res.T[None]
+    return out[0].T[None], out[1].T[None]
 
 
 def solution(mesh):

time: 152 us -> 147 us (0.967)
  Pallas kernels: 149 us -> 145 us
    pallas_call x1, Pallas kernels: 149 us -> 145 us  [shards(): pl.pallas_call(kernel, out_shape=jax.ShapeDtypeStruct((2, *tile), f32), i...]
    unnamed x2 -> x0, local copies, waits for them, and re-layouts: 2.75 us -> none
where the time goes in v5:
time: 147 us
  Pallas kernels  145 us (99%)
    pallas_call x1, Pallas kernels, shards(): pl.pallas_call(kernel, out_shape=jax.ShapeDtypeStruct((2, *tile), f32), i...  145 us

profile of v5, /device:TPU:1, one launch (start us, length us, event | category | flops | bytes accessed | tf_op | source)
XLA Modules:
  0.0 146.6 jit_solution(15021064120751534057)
XLA Ops:
  0.6 144.6 %broyden.1 = f32[2,64,128]{2,1,0:T(8,128)} custom-call(f32[1,64,128]{2,1,0:T(8,128)} %bitcast.22, f32[1,64,128]{2,1,0:T(8,128)} %bitcast.23, f32[1,8,64,128]{3,2,1,0:T(8,128)} %bitcast.19, f32[1,8,64,128]{3,2,1,0:T(8,128)} %bitcast.20, bf16[1,4,64,128]{3,2,1,0:T(8,128)(2,1)} %bitcast.21, bf16[1,4,2,128,1792]{4,3,2,1,0:T(8,128)(2,1)} %h_h.1, f32[1,64]{1,0:T(1,128)} %gain_h.1, ...), custom_call_target="tpu_custom_call" | custom-call | tf_op jit(solution)/shard_map/broyden/pallas_call | solution.py:520
  145.2 1.4 slice_bitcast_fusion

commit v6 on v5

--- a/solution.py
+++ b/solution.py
@@ -19,6 +19,7 @@
 PIECE = HID // ROW
 PARTS = 2
 PART = PIECE // PARTS
+STRIP = CHUNK // PARTS
 FAR_Z = (4, 3, 5, 2, 6, 1, 7)
 FAR_X = (2, 1, 3)
 FIRST_ORDER = [
@@ -314,9 +315,13 @@
             zs[m, pl.ds(4 * b, 4)] = part.astype(bf16).reshape(4, CHUNK, ROWS)
             if m == 0:
                 acc[rows] = part
-        for k in FAR_Z:
-            to = at_col(k)
-            remote(zs.at[m, to], zr.at[m, c], ss.at[6, m], rs.at[6, m], (s, r, to)).start()
+        for b in range(PARTS):
+            rows = pl.ds(b * STRIP, STRIP)
+            for k in FAR_Z:
+                to = at_col(k)
+                remote(
+                    zs.at[m, to, rows], zr.at[m, c, rows], ss.at[6, m], split.at[2, b, m], (s, r, to)
+                ).start()
         kzs[m] = inner
         for k in FAR_Z:
             remote(kzs.at[m], kzr.at[m, c], ss.at[8, m], rs.at[8, m], (s, r, at_col(k))).start()
@@ -349,22 +354,27 @@
             remote(dzs, dzr.at[c], one_s.at[6], one_r.at[6], (s, r, at_col(k))).start()
 
     def updated(m):
-        arrived(zr.at[m, pl.ds(0, COL - 1)], rs.at[6, m])
+        root = rstd[m]
+        for b in range(PARTS):
+            rows = pl.ds(b * STRIP, STRIP)
+            arrived(zr.at[m, pl.ds(0, COL - 1), rows], split.at[2, b, m])
+            total = jnp.sum(zr[m, :, rows].astype(f32), axis=0)
+            fresh = carry[m, rows] + root * (gain_t[rows] * total)
+            after[m, rows] = fresh
+
+            @pl.when(s != 0)
+            def _():
+                gys[m, rows] = fresh.astype(bf16)
+                for k in (*FAR_Z, 0):
+                    remote(
+                        gys.at[m, rows], gy.at[m, c, rows], ss.at[0, m], rs.at[0, m], (s - 1, r, at_col(k))
+                    ).start()
+
         arrived(kzr.at[m, pl.ds(0, COL - 1)], rs.at[8, m])
-        total = jnp.sum(zr[m].astype(f32), axis=0)
-        inner = jnp.sum(kzr[m], axis=0)
-        root = rstd[m]
-        fresh = carry[m] + root * (gain_t[...] * total)
-        after[m] = fresh
-        kps[m] = (root * root * root) * (inner / D)
+        kps[m] = (root * root * root) * (jnp.sum(kzr[m], axis=0) / D)
 
         @pl.when(s != 0)
         def _():
-            gys[m] = fresh.astype(bf16)
-            for k in (*FAR_Z, 0):
-                remote(
-                    gys.at[m], gy.at[m, c], ss.at[0, m], rs.at[0, m], (s - 1, r, at_col(k))
-                ).start()
             for k in range(ROW):
                 remote(kps.at[m], kpr.at[m, r], ss.at[7, m], rs.at[7, m], (s - 1, lax.rem(r + k, ROW), c)).start()
             remote(after.at[m], carry.at[m], ss.at[1, m], rs.at[1, m], (s - 1, r, c)).start()
@@ -372,7 +382,7 @@
         @pl.when(s == 0)
         def _():
             if m == 0:
-                home[...] = fresh
+                home[...] = after[m]
             else:
                 remote(after.at[m], home, ss.at[1, m], one_r.at[4], (m, r, c)).start()
                 for k in range(ROW):
@@ -582,7 +592,7 @@
             dma((2,)),
             dma((9, MB)),
             dma((9, MB)),
-            dma((2, PARTS, MB)),
+            dma((3, PARTS, MB)),
             dma((14,)),
             dma((14,)),
         ],

time: 147 us -> 141 us (0.959)
  Pallas kernels: 145 us -> 139 us
    pallas_call x1, Pallas kernels: 145 us -> 139 us  [shards(): pl.pallas_call(kernel, out_shape=jax.ShapeDtypeStruct((2, *tile), f32), i...]
where the time goes in v6:
time: 141 us
  Pallas kernels  139 us (99%)
    pallas_call x1, Pallas kernels, shards(): pl.pallas_call(kernel, out_shape=jax.ShapeDtypeStruct((2, *tile), f32), i...  139 us

profile of v6, /device:TPU:1, one launch (start us, length us, event | category | flops | bytes accessed | tf_op | source)
XLA Modules:
  0.0 140.7 jit_solution(14653323185271205646)
XLA Ops:
  0.6 138.7 %broyden.1 = f32[2,64,128]{2,1,0:T(8,128)} custom-call(f32[1,64,128]{2,1,0:T(8,128)} %bitcast.22, f32[1,64,128]{2,1,0:T(8,128)} %bitcast.23, f32[1,8,64,128]{3,2,1,0:T(8,128)} %bitcast.19, f32[1,8,64,128]{3,2,1,0:T(8,128)} %bitcast.20, bf16[1,4,64,128]{3,2,1,0:T(8,128)(2,1)} %bitcast.21, bf16[1,4,2,128,1792]{4,3,2,1,0:T(8,128)(2,1)} %h_h.1, f32[1,64]{1,0:T(1,128)} %gain_h.1, ...), custom_call_target="tpu_custom_call" | custom-call | tf_op jit(solution)/shard_map/broyden/pallas_call | solution.py:530
  139.3 1.4 slice_bitcast_fusion
